TPU v7x, 128 devices: a whole 4x4x4 slice. The times are simulated.
128 devices in a mesh: tm: 32 (over z_lo, x, y), panel: 4 (over z_hi, core).
Axes of the slice: x: 4, y: 4, z: 4 (z_hi: 2, z_lo: 2; z = z_hi * 2 + z_lo), core: 2. Of those that a mesh axis runs over, the one named last changes fastest.
Arguments:
- series: float32 [48, 8192], P(None, 'tm'), may hold values from -20 to 20, as said below
- start_block: float32 [18432, 64], P(('tm', 'panel')), may hold values from -6 to 6
Outputs:
- covariance: float32 [18432, 18432], P(('tm', 'panel'))
- basis: float32 [7, 18432, 64], P(None, ('tm', 'panel'))
- diag_blocks: float32 [6, 64, 64], replicated
- off_blocks: float32 [7, 64, 64], replicated
Inputs may be any that keep to these rules, and one draw needn't show every extreme that they name: `series`: each channel has its own scale.
All inputs are finite; a program needn't handle non-finite values.
Results may differ from a plain program's by a relative error of at most 0.0003.
Values sent between devices are 32-bit elements; how exact they have to be, the bound alone decides.
A program may use at most 128 MiB of HBM per device.

v0:
```python
import math

import jax
import jax.numpy as jnp
from jax import lax
from jax.sharding import PartitionSpec as P

M = 384
ITERS = 6


exact_precision = lax.Precision.HIGHEST


def passed_along(block, axis, distance):
    devices = range(lax.axis_size(axis))
    route = [(i - distance, i) for i in devices if i - distance in devices]
    return lax.ppermute(block, axis, route)


def gathered_total(x, axis):
    tiles = lax.all_gather(x, axis)
    return tiles.sum(axis=0)


def lag_block(local_rows, extended, first_lag, lag_width):
    day_count = local_rows.shape[1]
    span = day_count + lag_width - 1
    segment = extended[:, first_lag : first_lag + span]
    repeated = jnp.tile(segment, (1, lag_width + 1))[:, : lag_width * (span + 1)]
    windows = repeated.reshape(segment.shape[0], lag_width, span + 1)[:, :, :day_count]
    return jnp.einsum(
        "lt,mjt->ljm",
        local_rows,
        windows,
        precision=exact_precision,
        preferred_element_type=jnp.float32,
    )


def lag_products(local_rows, extended):
    lag_width = math.gcd(M, 128)
    parts_list = [
        lag_block(local_rows, extended, first_lag, lag_width)
        for first_lag in range(0, M, lag_width)
    ]
    return jnp.concatenate(parts_list, axis=1)


def local(series, start_block):
    channels, day_count = series.shape
    tm_size = lax.axis_size("tm")
    panel_size = lax.axis_size("panel")
    total_days = day_count * tm_size
    reach_hops = (M - 1 + day_count - 1) // day_count
    pieces = [series]
    moving = series
    for distance in range(reach_hops):
        moving = passed_along(moving, "tm", -1)
        pieces.append(moving)
    extended = jnp.concatenate(pieces, axis=1)
    summed = lax.psum(lag_products(series, extended), "tm")
    counts = (total_days - jnp.arange(M)).astype(jnp.float32)
    normed = summed / counts[None, :, None]
    two_sided = jnp.concatenate([jnp.transpose(normed, (2, 1, 0))[:, :0:-1, :], normed], axis=1)
    lags_here = M // (tm_size * panel_size)
    block_index = lax.axis_index("tm") * panel_size + lax.axis_index("panel")
    row_list = []
    for offset in range(lags_here):
        lag_index = block_index * lags_here + offset
        window = lax.dynamic_slice(
            two_sided, (jnp.int32(0), M - 1 - lag_index, jnp.int32(0)), (channels, M, channels)
        )
        row_list.append(window.reshape(channels, M * channels))
    covariance = jnp.concatenate(row_list, axis=0)

    def inner(left, right):
        return jnp.dot(left.T, right, precision=exact_precision, preferred_element_type=jnp.float32)

    factor = jnp.linalg.cholesky(gathered_total(inner(start_block, start_block), ("tm", "panel")))
    current = jax.scipy.linalg.solve_triangular(factor, start_block.T, lower=True).T
    previous = jnp.zeros_like(current)
    upper = factor.T
    basis_list = [current]
    diagonal_list = []
    upper_list = [upper]
    for iteration in range(ITERS):
        work = jnp.dot(
            covariance,
            lax.all_gather(current, ("tm", "panel"), axis=0, tiled=True),
            precision=exact_precision,
            preferred_element_type=jnp.float32,
        )
        if iteration > 0:
            work = work - jnp.dot(
                previous, upper.T, precision=exact_precision, preferred_element_type=jnp.float32
            )
        diagonal, work_gram, basis_gram = lax.psum(
            (inner(current, work), inner(work, work), inner(current, current)), ("tm", "panel")
        )
        work = work - jnp.dot(
            current, diagonal, precision=exact_precision, preferred_element_type=jnp.float32
        )
        cross_term = jnp.dot(
            diagonal.T, diagonal, precision=exact_precision, preferred_element_type=jnp.float32
        )
        weighted = jnp.dot(
            diagonal.T,
            jnp.dot(
                basis_gram, diagonal, precision=exact_precision, preferred_element_type=jnp.float32
            ),
            precision=exact_precision,
            preferred_element_type=jnp.float32,
        )
        gram_matrix = work_gram - 2.0 * cross_term + weighted
        factor = jnp.linalg.cholesky(gram_matrix)
        upper = factor.T
        previous = current
        current = jax.scipy.linalg.solve_triangular(factor, work.T, lower=True).T
        basis_list.append(current)
        diagonal_list.append(diagonal)
        upper_list.append(upper)
    return (covariance, jnp.stack(basis_list), jnp.stack(diagonal_list), jnp.stack(upper_list))


def solution(mesh):
    placed = (P(None, "tm"), P(("tm", "panel"), None))
    return jax.shard_map(
        local,
        mesh=mesh,
        in_specs=placed,
        out_specs=(P(("tm", "panel"), None), P(None, ("tm", "panel"), None), P(), P()),
        check_vma=False,
    )
```

profile of v0, /device:TPU:1, one launch (start us, length us, event | category | flops | bytes accessed | tf_op | source)
XLA Modules:
  0.0 2211.1 jit_solution(17596680052588923745)
XLA Ops:
  108.8 106.1 %all-gather.15.cloned.1.call-done = f32[8192,64]{1,0:T(8,128)} async-done(((f32[64,64]{1,0:T(8,128)}), f32[8192,64]{1,0:T(8,128)}) %all-gather.15.cloned.1.call-update) | async-done | bytes 2097168 | tf_op jit(solution)/shard_map/all_gather | solution.py:22
  231.0 185.9 %all-reduce.8.cloned.1.call-done = f32[48,384,48]{1,0,2:T(8,128)} async-done(((f32[48,384,48]{1,0,2:T(8,128)}), f32[48,384,48]{1,0,2:T(8,128)}) %all-reduce.8.cloned.1.call-update) | async-done | bytes 3538960 | tf_op jit(solution)/shard_map/psum | solution.py:62
  504.1 11.5 copy.74
  525.3 14.1 fusion.82
  539.8 85.4 %all-reduce.5 = (f32[64,64]{1,0:T(8,128)S(1)}, f32[64,64]{0,1:T(8,128)S(1)}, f32[64,64]{1,0:T(8,128)S(1)}) all-reduce(f32[64,64]{1,0:T(8,128)S(1)} %fusion.84, f32[64,64]{0,1:T(8,128)S(1)} %fusion.83, f32[64,64]{1,0:T(8,128)S(1)} %fusion.85), channel_id=1, replica_groups=mesh['tm'=32,'panel'=4] {'tm','panel'}, use_global_device_ids=true, to_apply=%region_5.0 | all-reduce | flops 12288 | bytes 98304 | tf_op jit(solution)/shard_map/psum | solution.py:98
  641.3 196.9 %all-gather.19.cloned.1.call-done = f32[128,144,64]{1,2,0:T(8,128)} async-done(((f32[1,144,64]{1,2,0:T(8,128)}), f32[128,144,64]{1,2,0:T(8,128)}) %all-gather.19.cloned.1.call-update) | async-done | bytes 4718608 | tf_op jit(solution)/shard_map/all_gather | solution.py:90
  838.2 11.5 copy.79
  859.8 14.1 convolution_subtract_fusion.4
  874.4 63.9 %all-reduce.4 = (f32[64,64]{1,0:T(8,128)S(1)}, f32[64,64]{0,1:T(8,128)S(1)}, f32[64,64]{1,0:T(8,128)S(1)}) all-reduce(f32[64,64]{1,0:T(8,128)S(1)} %fusion.88, f32[64,64]{0,1:T(8,128)S(1)} %fusion.87, f32[64,64]{1,0:T(8,128)S(1)} %fusion.89), channel_id=1, replica_groups=mesh['tm'=32,'panel'=4] {'tm','panel'}, use_global_device_ids=true, to_apply=%region_8.0 | all-reduce | flops 12288 | bytes 98304 | tf_op jit(solution)/shard_map/psum | solution.py:98
  954.5 196.1 %all-gather.21.cloned.1.call-done = f32[128,144,64]{1,2,0:T(8,128)} async-done(((f32[1,144,64]{1,2,0:T(8,128)}), f32[128,144,64]{1,2,0:T(8,128)}) %all-gather.21.cloned.1.call-update) | async-done | bytes 4718608 | tf_op jit(solution)/shard_map/all_gather | solution.py:90
  1150.6 11.5 copy.84
  1171.8 14.1 convolution_subtract_fusion.3
  1186.4 64.0 %all-reduce.3 = (f32[64,64]{1,0:T(8,128)S(1)}, f32[64,64]{0,1:T(8,128)S(1)}, f32[64,64]{1,0:T(8,128)S(1)}) all-reduce(f32[64,64]{1,0:T(8,128)S(1)} %fusion.92, f32[64,64]{0,1:T(8,128)S(1)} %fusion.91, f32[64,64]{1,0:T(8,128)S(1)} %fusion.93), channel_id=1, replica_groups=mesh['tm'=32,'panel'=4] {'tm','panel'}, use_global_device_ids=true, to_apply=%region_11.0 | all-reduce | flops 12288 | bytes 98304 | tf_op jit(solution)/shard_map/psum | solution.py:98
  1266.9 196.0 %all-gather.23.cloned.1.call-done = f32[128,144,64]{1,2,0:T(8,128)} async-done(((f32[1,144,64]{1,2,0:T(8,128)}), f32[128,144,64]{1,2,0:T(8,128)}) %all-gather.23.cloned.1.call-update) | async-done | bytes 4718608 | tf_op jit(solution)/shard_map/all_gather | solution.py:90
  1484.0 14.1 convolution_subtract_fusion.2
  1498.6 64.1 %all-reduce.2 = (f32[64,64]{1,0:T(8,128)S(1)}, f32[64,64]{0,1:T(8,128)S(1)}, f32[64,64]{1,0:T(8,128)S(1)}) all-reduce(f32[64,64]{1,0:T(8,128)S(1)} %fusion.96, f32[64,64]{0,1:T(8,128)S(1)} %fusion.95, f32[64,64]{1,0:T(8,128)S(1)} %fusion.97), channel_id=1, replica_groups=mesh['tm'=32,'panel'=4] {'tm','panel'}, use_global_device_ids=true, to_apply=%region_14.0 | all-reduce | flops 12288 | bytes 98304 | tf_op jit(solution)/shard_map/psum | solution.py:98
  1578.9 196.4 %all-gather.25.cloned.1.call-done = f32[128,144,64]{1,2,0:T(8,128)} async-done(((f32[1,144,64]{1,2,0:T(8,128)}), f32[128,144,64]{1,2,0:T(8,128)}) %all-gather.25.cloned.1.call-update) | async-done | bytes 4718608 | tf_op jit(solution)/shard_map/all_gather | solution.py:90
  1775.3 11.5 copy.94
  1796.5 14.1 convolution_subtract_fusion.1
  1811.0 64.1 %all-reduce.1 = (f32[64,64]{1,0:T(8,128)S(1)}, f32[64,64]{0,1:T(8,128)S(1)}, f32[64,64]{1,0:T(8,128)S(1)}) all-reduce(f32[64,64]{1,0:T(8,128)S(1)} %fusion.100, f32[64,64]{0,1:T(8,128)S(1)} %fusion.99, f32[64,64]{1,0:T(8,128)S(1)} %fusion.101), channel_id=1, replica_groups=mesh['tm'=32,'panel'=4] {'tm','panel'}, use_global_device_ids=true, to_apply=%region_17.0 | all-reduce | flops 12288 | bytes 98304 | tf_op jit(solution)/shard_map/psum | solution.py:98
  1894.9 192.7 %all-gather.27.cloned.1.call-done = f32[128,144,64]{1,2,0:T(8,128)} async-done(((f32[1,144,64]{1,2,0:T(8,128)}), f32[128,144,64]{1,2,0:T(8,128)}) %all-gather.27.cloned.1.call-update) | async-done | bytes 4718608 | tf_op jit(solution)/shard_map/all_gather | solution.py:90
  2087.6 11.5 copy.99
  2108.7 14.3 convolution_subtract_fusion
  2123.5 64.0 %all-reduce = (f32[64,64]{1,0:T(8,128)S(1)}, f32[64,64]{0,1:T(8,128)S(1)}, f32[64,64]{1,0:T(8,128)S(1)}) all-reduce(f32[64,64]{1,0:T(8,128)S(1)} %fusion.104, f32[64,64]{0,1:T(8,128)S(1)} %fusion.103, f32[64,64]{1,0:T(8,128)S(1)} %fusion.105), channel_id=1, replica_groups=mesh['tm'=32,'panel'=4] {'tm','panel'}, use_global_device_ids=true, to_apply=%region_20.23 | all-reduce | flops 12288 | bytes 98304 | tf_op jit(solution)/shard_map/psum | solution.py:98
  (227 shorter events, 376.3 us)
Async XLA Ops:
  8.0 206.8 %all-gather.15.cloned.1.call-start = ((), (), s32[]{:S(2)}) async-start(), calls=%async_computation.1 | async-start | bytes 4227072 | tf_op jit(solution)/shard_map/all_gather | solution.py:22
  9.7 407.1 %all-reduce.8.cloned.1.call-start = ((), (), s32[]{:S(2)}) async-start(), calls=%async_computation | async-start | bytes 7077888 | tf_op jit(solution)/shard_map/psum | solution.py:62
  9.7 5.7 collective-permute-start
  53.2 10.4 slice-start.3
  53.2 10.4 slice-start.4
  56.9 6.7 slice-start.5
  56.9 6.7 copy-start.14
  62.3 18.5 collective-permute-start.1
  100.5 6.1 copy-start.6
  100.5 6.1 copy-start.7
  108.7 395.4 %all-gather.17.cloned.1.call-start = ((), (), s32[]{:S(2)}) async-start(), calls=%async_computation.2 | async-start | bytes 8454144 | tf_op jit(solution)/shard_map/all_gather | solution.py:90
  230.5 607.7 %all-gather.19.cloned.1.call-start = ((), (), s32[]{:S(2)}) async-start(), calls=%async_computation.3 | async-start | bytes 8454144 | tf_op jit(solution)/shard_map/all_gather | solution.py:90
  495.6 4.2 copy-start.4
  495.6 6.2 copy-start.5
  639.2 511.4 %all-gather.21.cloned.1.call-start = ((), (), s32[]{:S(2)}) async-start(), calls=%async_computation.4 | async-start | bytes 8454144 | tf_op jit(solution)/shard_map/all_gather | solution.py:90
  859.8 14.1 copy-start.10
  952.2 510.6 %all-gather.23.cloned.1.call-start = ((), (), s32[]{:S(2)}) async-start(), calls=%async_computation.5 | async-start | bytes 8454144 | tf_op jit(solution)/shard_map/all_gather | solution.py:90
  1171.8 14.1 copy-start.11
  1264.4 510.9 %all-gather.25.cloned.1.call-start = ((), (), s32[]{:S(2)}) async-start(), calls=%async_computation.6 | async-start | bytes 8454144 | tf_op jit(solution)/shard_map/all_gather | solution.py:90
  1484.0 14.1 copy-start.12
  1576.8 510.8 %all-gather.27.cloned.1.call-start = ((), (), s32[]{:S(2)}) async-start(), calls=%async_computation.7 | async-start | bytes 8454144 | tf_op jit(solution)/shard_map/all_gather | solution.py:90
  1796.5 14.1 copy-start.9
  2099.0 104.2 %copy-start.1 = (f32[144,64]{0,1:T(8,128)S(1)}, f32[144,64]{0,1:T(8,128)}, u32[]{:S(2)}) copy-start(f32[144,64]{0,1:T(8,128)} %param.6) | copy-start | bytes 110596
  2108.7 14.3 copy-start.13
  (9 other events, 25.7 us)
Sparse Core Ops, SparseCore 0:
  11.1 203.6 all-gather.14
  230.6 202.9 all-gather.16
  639.3 198.8 all-gather.18
  952.4 198.2 all-gather.20
  1264.5 198.2 all-gather.22
  1576.9 198.3 all-gather.24
  1889.1 198.3 all-gather.26
Sparse Core Ops, SparseCore 1:
  108.8 308.0 all-reduce.7
where the time goes:
time: 2220 us; the launch traced here: 2210 us
  waiting for transfers between devices  1270 us (57%)
  blocking collectives  405 us (18%)
  local copies, waits for them, and re-layouts  274 us (12%)
  matrix products  133 us (6%)
  other arithmetic  104 us (5%)
    all_gather x6, waiting for transfers between devices, local(): lax.all_gather(current, ('tm', 'panel'), axis=0, tiled=True)  978 us
    psum x6, blocking collectives, local(): lax.psum((inner(current, work), inner(work, work), inner(current, current...  405 us
    psum x1, waiting for transfers between devices, local(): summed = lax.psum(lag_products(series, extended), 'tm')  186 us
    all_gather x1, waiting for transfers between devices, gathered_total(): tiles = lax.all_gather(x, axis)  106 us
    unnamed x60, local copies, waits for them, and re-layouts  91.1 us
    dot_general x6, matrix products, local(): jnp.dot(covariance, lax.all_gather(current, ('tm', 'panel'), axis=0, tile...  84.9 us
    all_gather x6, local copies, waits for them, and re-layouts, local(): lax.all_gather(current, ('tm', 'panel'), axis=0, tiled=True)  68.7 us
  transfers between devices with their start and end apart: 10, of which 8 were waited for; matrix products, arithmetic and copies ran while one was open for 9% of the time, Pallas kernels for 0%

commit v1 on v0

v1 whole, which is shorter than its diff:
```python
import functools
import math

import jax
import jax.numpy as jnp
from jax import lax
from jax.experimental import pallas as pl
from jax.experimental.pallas import tpu as pltpu
from jax.sharding import PartitionSpec as P

L = 48
M = 384
B = 64
ITERS = 6
ROWS = 144
HALF = ROWS // 2
PLANE = 16
LINE = 8
COLS = PLANE * ROWS

exact_precision = lax.Precision.HIGHEST
MESH = pl.DeviceIdType.MESH


def passed_along(block, axis, distance):
    devices = range(lax.axis_size(axis))
    route = [(i - distance, i) for i in devices if i - distance in devices]
    return lax.ppermute(block, axis, route)


def lag_block(local_rows, extended, first_lag, lag_width):
    day_count = local_rows.shape[1]
    span = day_count + lag_width - 1
    segment = extended[:, first_lag : first_lag + span]
    repeated = jnp.tile(segment, (1, lag_width + 1))[:, : lag_width * (span + 1)]
    windows = repeated.reshape(segment.shape[0], lag_width, span + 1)[:, :, :day_count]
    return jnp.einsum(
        "lt,mjt->ljm",
        local_rows,
        windows,
        precision=exact_precision,
        preferred_element_type=jnp.float32,
    )


def lag_products(local_rows, extended):
    lag_width = math.gcd(M, 128)
    parts_list = [
        lag_block(local_rows, extended, first_lag, lag_width)
        for first_lag in range(0, M, lag_width)
    ]
    return jnp.concatenate(parts_list, axis=1)


def split3(x):
    hi = x.astype(jnp.bfloat16)
    rest = x - hi.astype(jnp.float32)
    mid = rest.astype(jnp.bfloat16)
    low = (rest - mid.astype(jnp.float32)).astype(jnp.bfloat16)
    return hi, mid, low


def assemble_kernel(window_ref, hi_ref, mid_ref, low_ref):
    for offset in range(12):
        pieces = [
            window_ref[0, :, L * (11 - offset + 12 * plane) : L * (11 - offset + 12 * plane) + ROWS]
            for plane in range(PLANE)
        ]
        rows = jnp.concatenate(pieces, axis=1)
        hi, mid, low = split3(rows)
        at = slice(L * offset, L * offset + L)
        hi_ref[0, at, :] = hi
        mid_ref[0, at, :] = mid
        low_ref[0, at, :] = low


def assemble(windows):
    width = windows.shape[2]
    shape = jax.ShapeDtypeStruct((2, 12 * L, COLS), jnp.bfloat16)
    spec = pl.BlockSpec((1, 12 * L, COLS), lambda h: (h, 0, 0))
    return pl.pallas_call(
        assemble_kernel,
        grid=(2,),
        out_shape=(shape, shape, shape),
        in_specs=[pl.BlockSpec((1, L, width), lambda h: (h, 0, 0))],
        out_specs=(spec, spec, spec),
        compiler_params=pltpu.CompilerParams(vmem_limit_bytes=60 * 1024 * 1024),
    )(windows)


def exact_dot(left, right, contract):
    return lax.dot_general(
        left,
        right,
        (contract, ((), ())),
        precision=exact_precision,
        preferred_element_type=jnp.float32,
    )


def factor(gram):
    rows = lax.broadcasted_iota(jnp.int32, (B, 2 * B), 0)
    lanes = lax.broadcasted_iota(jnp.int32, (B, 2 * B), 1)
    small_rows = lax.broadcasted_iota(jnp.int32, (B, B), 0)
    small_lanes = lax.broadcasted_iota(jnp.int32, (B, B), 1)
    identity = jnp.where(small_rows == small_lanes, 1.0, 0.0).astype(jnp.float32)
    work = jnp.concatenate([gram, identity], axis=1)
    width = 4
    for first in range(0, B, width):
        columns = [
            jnp.broadcast_to(work[:, first + t : first + t + 1], (B, 2 * B)) for t in range(width)
        ]
        for t in range(width):
            k = first + t
            column = columns[t]
            scale = 1.0 / column[k : k + 1, :]
            weight = jnp.where(rows > k, column * scale, 0.0)
            work = work - weight * work[k : k + 1, :]
            for u in range(t + 1, width):
                columns[u] = columns[u] - weight * column[first + u : first + u + 1, :]
    pivots = jnp.sum(jnp.where(rows == lanes, work, 0.0), axis=1, keepdims=True)
    scaled = work * lax.rsqrt(pivots)
    upper = jnp.where(small_lanes >= small_rows, scaled[:, :B], 0.0)
    inverse = jnp.where(small_lanes <= small_rows, scaled[:, B:], 0.0)
    return upper, inverse


def lanczos_kernel(
    start_ref,
    hi_ref,
    mid_ref,
    low_ref,
    basis_ref,
    diag_ref,
    off_ref,
    work,
    current,
    packed,
    gathered,
    stacked,
    partial,
    landed,
    gram,
    stage1,
    slab,
    stage2,
    total,
    full,
    send_q,
    recv_q,
    send_p,
    recv_p,
    send_1,
    recv_1,
    send_2,
    recv_2,
    send_3,
    recv_3,
):
    tm = lax.axis_index("tm")
    panel = lax.axis_index("panel")
    low_z = tm // PLANE
    plane = tm % PLANE
    line = low_z * 4 + panel

    def plane_peer(step):
        spot_x = (plane // 4 + step // 4) % 4
        spot_y = (plane % 4 + step % 4) % 4
        spot = spot_x * 4 + spot_y
        return spot, (low_z * PLANE + spot, panel)

    def line_peer(step):
        spot_z = (low_z + step // 4) % 2
        spot_p = (panel + step % 4) % 4
        return spot_z * 4 + spot_p, (spot_z * PLANE + plane, spot_p)

    barrier = pltpu.get_barrier_semaphore()
    for step in range(1, PLANE):
        pl.semaphore_signal(barrier, inc=1, device_id=plane_peer(step)[1], device_id_type=MESH)
    for step in range(1, LINE):
        pl.semaphore_signal(barrier, inc=1, device_id=line_peer(step)[1], device_id_type=MESH)
    pl.semaphore_wait(barrier, PLANE + LINE - 2)

    def plane_copy(step, source, target, sends, receives):
        spot, device = plane_peer(step)
        return pltpu.make_async_remote_copy(
            src_ref=source,
            dst_ref=target.at[plane],
            send_sem=sends.at[step],
            recv_sem=receives.at[step],
            device_id=device,
            device_id_type=MESH,
        )

    def line_copy(step, source, target, sends, receives):
        return pltpu.make_async_remote_copy(
            src_ref=source,
            dst_ref=target,
            send_sem=sends.at[step],
            recv_sem=receives.at[step],
            device_id=line_peer(step)[1],
            device_id_type=MESH,
        )

    def gram_total(basis_block, rows_block):
        both = jnp.concatenate([basis_block, rows_block], axis=1)
        gram[...] = exact_dot(both, both, ((0,), (0,))).reshape(LINE, 16, 2 * B)
        firsts = [
            line_copy(step, gram.at[line_peer(step)[0]], stage1.at[line], send_1, recv_1)
            for step in range(1, LINE)
        ]
        for copy in firsts:
            copy.start()
        stage1[line] = gram[line]
        for copy in firsts:
            copy.wait()
        reduced = stage1[0]
        for spot in range(1, LINE):
            reduced = reduced + stage1[spot]
        slab[...] = reduced
        stage2[plane] = reduced
        seconds = [plane_copy(step, slab, stage2, send_2, recv_2) for step in range(1, PLANE)]
        for copy in seconds:
            copy.start()
        for copy in seconds:
            copy.wait()
        reduced = stage2[0]
        for spot in range(1, PLANE):
            reduced = reduced + stage2[spot]
        total[...] = reduced
        full[line] = reduced
        thirds = [line_copy(step, total, full.at[line], send_3, recv_3) for step in range(1, LINE)]
        for copy in thirds:
            copy.start()
        for copy in thirds:
            copy.wait()
        return full[...].reshape(2 * B, 2 * B)

    work[...] = start_ref[...]
    current[...] = jnp.zeros_like(current)

    def one_step(step_at, carry):
        summed = gram_total(current[...], work[...])
        basis_gram = summed[:B, :B]
        diagonal = summed[:B, B:]
        work_gram = summed[B:, B:]
        weighted = exact_dot(basis_gram, diagonal, ((1,), (0,)))
        left = exact_dot(diagonal, 2.0 * diagonal - weighted, ((0,), (0,)))
        upper, inverse = factor(work_gram - left)
        reduced = work[...] - exact_dot(current[...], diagonal, ((1,), (0,)))
        fresh = exact_dot(reduced, inverse, ((1,), (1,)))
        diag_ref[step_at] = diagonal
        off_ref[step_at] = upper
        basis_ref[step_at] = fresh

        @pl.when(step_at < ITERS)
        def _():
            block = jnp.concatenate([fresh[:HALF], fresh[HALF:]], axis=1)
            packed[...] = block
            gathered[plane] = block
            copies = [plane_copy(step, packed, gathered, send_q, recv_q) for step in range(1, PLANE)]
            for copy in copies:
                copy.start()
            back = exact_dot(current[...], upper, ((1,), (1,)))
            current[...] = fresh
            for copy in copies:
                copy.wait()

            def unpack(spot, carry):
                block = gathered[spot]
                block = jnp.concatenate([block[:, :B], block[:, B:]], axis=0)
                hi, mid, low = split3(block)
                at = pl.ds(pl.multiple_of(spot * ROWS, ROWS), ROWS)
                stacked[at, :] = jnp.concatenate([hi, mid, low], axis=1)
                return carry

            lax.fori_loop(0, PLANE, unpack, 0)

            def multiply(h, carry):
                first = jnp.dot(hi_ref[h], stacked[...], preferred_element_type=jnp.float32)
                second = jnp.dot(
                    mid_ref[h], stacked[:, : 2 * B], preferred_element_type=jnp.float32
                )
                third = jnp.dot(low_ref[h], stacked[:, :B], preferred_element_type=jnp.float32)
                low_part = third + second[:, B:] + first[:, 2 * B :]
                product = first[:, :B] + (first[:, B : 2 * B] + second[:, :B] + low_part)
                for spot in range(4):
                    rows = product[spot * ROWS : (spot + 1) * ROWS]
                    partial[h * 4 + spot] = jnp.concatenate([rows[:HALF], rows[HALF:]], axis=1)
                return carry

            lax.fori_loop(0, 2, multiply, 0)
            sums = [
                line_copy(step, partial.at[line_peer(step)[0]], landed.at[line], send_p, recv_p)
                for step in range(1, LINE)
            ]
            for copy in sums:
                copy.start()
            landed[line] = partial[line]
            for copy in sums:
                copy.wait()
            value = landed[0]
            for spot in range(1, LINE):
                value = value + landed[spot]
            work[...] = jnp.concatenate([value[:, :B], value[:, B:]], axis=0) - back

        return carry

    lax.fori_loop(0, ITERS + 1, one_step, 0)


def lanczos(start, hi, mid, low):
    vmem = pl.BlockSpec(memory_space=pltpu.VMEM)
    dma = pltpu.SemaphoreType.DMA
    return pl.pallas_call(
        lanczos_kernel,
        out_shape=(
            jax.ShapeDtypeStruct((ITERS + 1, ROWS, B), jnp.float32),
            jax.ShapeDtypeStruct((ITERS + 1, B, B), jnp.float32),
            jax.ShapeDtypeStruct((ITERS + 1, B, B), jnp.float32),
        ),
        in_specs=[vmem] * 4,
        out_specs=(vmem, vmem, vmem),
        scratch_shapes=[
            pltpu.VMEM((ROWS, B), jnp.float32),
            pltpu.VMEM((ROWS, B), jnp.float32),
            pltpu.VMEM((HALF, 2 * B), jnp.float32),
            pltpu.VMEM((PLANE, HALF, 2 * B), jnp.float32),
            pltpu.VMEM((COLS, 3 * B), jnp.bfloat16),
            pltpu.VMEM((LINE, HALF, 2 * B), jnp.float32),
            pltpu.VMEM((LINE, HALF, 2 * B), jnp.float32),
            pltpu.VMEM((LINE, 16, 2 * B), jnp.float32),
            pltpu.VMEM((LINE, 16, 2 * B), jnp.float32),
            pltpu.VMEM((16, 2 * B), jnp.float32),
            pltpu.VMEM((PLANE, 16, 2 * B), jnp.float32),
            pltpu.VMEM((16, 2 * B), jnp.float32),
            pltpu.VMEM((LINE, 16, 2 * B), jnp.float32),
            dma((PLANE,)),
            dma((PLANE,)),
            dma((LINE,)),
            dma((LINE,)),
            dma((LINE,)),
            dma((LINE,)),
            dma((PLANE,)),
            dma((PLANE,)),
            dma((LINE,)),
            dma((LINE,)),
        ],
        compiler_params=pltpu.CompilerParams(
            collective_id=0, has_side_effects=True, vmem_limit_bytes=60 * 1024 * 1024
        ),
    )(start, hi, mid, low)


def local(series, start_block):
    channels, day_count = series.shape
    tm_size = lax.axis_size("tm")
    panel_size = lax.axis_size("panel")
    total_days = day_count * tm_size
    reach_hops = (M - 1 + day_count - 1) // day_count
    pieces = [series]
    moving = series
    for distance in range(reach_hops):
        moving = passed_along(moving, "tm", -1)
        pieces.append(moving)
    extended = jnp.concatenate(pieces, axis=1)
    summed = lax.psum(lag_products(series, extended), "tm")
    counts = (total_days - jnp.arange(M)).astype(jnp.float32)
    normed = summed / counts[None, :, None]
    two_sided = jnp.concatenate([jnp.transpose(normed, (2, 1, 0))[:, :0:-1, :], normed], axis=1)
    flat = two_sided.reshape(channels, (2 * M - 1) * channels)
    tm = lax.axis_index("tm")
    panel = lax.axis_index("panel")
    block_index = tm * panel_size + panel
    covariance = jnp.concatenate(
        [
            lax.dynamic_slice(
                flat, (0, (M - 1 - 3 * block_index - offset) * channels), (channels, M * channels)
            )
            for offset in range(3)
        ],
        axis=0,
    )
    windows = jnp.stack(
        [
            lax.dynamic_slice(
                flat,
                (0, (372 + (tm // PLANE - h) * 192 - 12 * (tm % PLANE) + 3 * panel) * channels),
                (channels, 194 * channels),
            )
            for h in range(2)
        ]
    )
    hi, mid, low = assemble(windows)
    basis, diag, off = lanczos(start_block, hi, mid, low)
    return covariance, basis, diag[1:], off


def solution(mesh):
    placed = (P(None, "tm"), P(("tm", "panel"), None))
    return jax.shard_map(
        local,
        mesh=mesh,
        in_specs=placed,
        out_specs=(P(("tm", "panel"), None), P(None, ("tm", "panel"), None), P(), P()),
        check_vma=False,
    )
```

time: 2220 us -> 793 us (0.36)
  waiting for transfers between devices: 1270 us -> 310 us
  blocking collectives: 405 us -> 0 us
  Pallas kernels: 0 us -> 293 us
  local copies, waits for them, and re-layouts: 274 us -> 123 us
  matrix products: 133 us -> 20.3 us
  other arithmetic: 104 us -> 15.2 us
    all_gather x7 -> x0, waiting for transfers between devices: 1080 us -> none  [the longest x6 978 us: local(): lax.all_gather(current, ('tm', 'panel'), axis=0, tiled=True)]
    psum x6 -> x0, blocking collectives: 405 us -> none  [local(): lax.psum((inner(current, work), inner(work, work), inner(current, current...]
    pallas_call x0 -> x2, Pallas kernels: none -> 293 us  [the longest x1 283 us: lanczos(): pl.pallas_call(lanczos_kernel, out_shape=(jax.ShapeDtypeStruct((ITERS + 1...]
    psum x1, waiting for transfers between devices: 186 us -> 306 us  [local(): summed = lax.psum(lag_products(series, extended), 'tm')]
    dot_general x54 -> x0, matrix products: 104 us -> none  [the longest x6 84.9 us: local(): jnp.dot(covariance, lax.all_gather(current, ('tm', 'panel'), axis=0, tile...]
    another operation x36 -> x1, other arithmetic: 85.1 us -> 2.07 us  [local(): jnp.stack([lax.dynamic_slice(flat, (0, (372 + (tm // PLANE - h) * 192 - 1...]
    unnamed x60 -> x19, local copies, waits for them, and re-layouts: 91.1 us -> 20.6 us
    all_gather x6 -> x0, local copies, waits for them, and re-layouts: 68.7 us -> none  [local(): lax.all_gather(current, ('tm', 'panel'), axis=0, tiled=True)]
  transfers between devices with their start and end apart: 10 -> 3, of which waited for: 8 -> 2; matrix products, arithmetic and copies ran while one was open for 9% -> 1% of each run, Pallas kernels for 0% -> 0%
where the time goes in v1:
time: 793 us; the launch traced here: 779 us
  waiting for transfers between devices  310 us (39%)
  Pallas kernels  293 us (37%)
  local copies, waits for them, and re-layouts  123 us (16%)
  matrix products  20.3 us (3%)
  other arithmetic  15.2 us (2%)
  between operations  14.4 us (2%)
    psum x1, waiting for transfers between devices, local(): summed = lax.psum(lag_products(series, extended), 'tm')  306 us
    pallas_call x1, Pallas kernels, lanczos(): pl.pallas_call(lanczos_kernel, out_shape=(jax.ShapeDtypeStruct((ITERS + 1...  283 us
    another operation x6, local copies, waits for them, and re-layouts, lag_block(): repeated = jnp.tile(segment, (1, lag_width + 1))[:, :lag_width * (span + 1)]  43.1 us
    unnamed x19, local copies, waits for them, and re-layouts  20.6 us
    dot_general x3, matrix products, lag_block(): jnp.einsum('lt,mjt->ljm', local_rows, windows, precision=exact_precision,...  20.3 us
    reshape x1, local copies, waits for them, and re-layouts, local(): flat = two_sided.reshape(channels, (2 * M - 1) * channels)  19.5 us
  transfers between devices with their start and end apart: 3, of which 2 were waited for; matrix products, arithmetic and copies ran while one was open for 1% of the time, Pallas kernels for 0%

profile of v1, /device:TPU:1, one launch (start us, length us, event | category | flops | bytes accessed | tf_op | source)
XLA Modules:
  0.0 778.8 jit_solution(1148939951113714777)
XLA Ops:
  9.3 3.6 collective-permute-done
  12.9 4.6 tile.12
  17.5 9.8 %tile.13 = f32[48,49407]{1,0:T(8,128)} reshape(f32[48,129,383]{2,1,0:T(8,128)} %tile.12) | data formatting | bytes 18972288 | tf_op jit(solution)/shard_map/tile | solution.py:35
  27.3 3.7 slice-done
  32.6 7.1 fusion.6
  39.8 4.6 tile.14
  44.3 9.8 %tile.30 = f32[48,49407]{1,0:T(8,128)} reshape(f32[48,129,383]{2,1,0:T(8,128)} %tile.14) | data formatting | bytes 18972288 | tf_op jit(solution)/shard_map/tile | solution.py:35
  54.1 3.7 slice-done.1
  61.1 7.1 fusion.9
  68.2 4.6 tile.31
  72.8 9.8 %tile.32 = f32[48,49407]{1,0:T(8,128)} reshape(f32[48,129,383]{2,1,0:T(8,128)} %tile.31) | data formatting | bytes 18972288 | tf_op jit(solution)/shard_map/tile | solution.py:35
  82.6 3.7 slice-done.2
  87.9 6.1 fusion.12
  97.6 306.3 %all-reduce.2.cloned.1.call-done = f32[48,384,48]{1,0,2:T(8,128)} async-done(((f32[48,384,48]{1,0,2:T(8,128)}), f32[48,384,48]{1,0,2:T(8,128)}) %all-reduce.2.cloned.1.call-update) | async-done | bytes 3538960 | tf_op jit(solution)/shard_map/psum | solution.py:367
  410.1 7.6 reverse
  417.8 3.0 slice.68
  420.7 4.4 pad_maximum_fusion.1
  425.2 13.1 %copy.10 = f32[48,767,48]{2,1,0:T(8,128)} copy(f32[48,767,48]{1,0,2:T(8,128)} %pad_maximum_fusion.1) | data formatting | bytes 14137344 | tf_op jit(solution)/shard_map/concatenate | solution.py:370
  438.3 19.5 %reshape.40 = f32[48,36816]{1,0:T(8,128)} reshape(f32[48,767,48]{2,1,0:T(8,128)} %copy.10) | data formatting | bytes 14137344 | tf_op jit(solution)/shard_map/reshape | solution.py:371
  457.8 3.0 dynamic-slice_bitcast_fusion.1
  462.9 9.3 %shard_map.57 = (bf16[2,576,2304]{2,1,0:T(8,128)(2,1)}, bf16[2,576,2304]{2,1,0:T(8,128)(2,1)}, bf16[2,576,2304]{2,1,0:T(8,128)(2,1)}) custom-call(f32[2,48,9312]{2,1,0:T(8,128)} %pad_maximum_fusion.2.window_ref), custom_call_target="tpu_custom_call" | custom-call | tf_op jit(solution)/shard_map/pallas_call | solution.py:81
  472.3 283.5 %shard_map.58 = (f32[7,144,64]{2,1,0:T(8,128)}, f32[7,64,64]{2,1,0:T(8,128)}, f32[7,64,64]{2,1,0:T(8,128)}) custom-call(f32[144,64]{1,0:T(8,128)} %copy.11.start_ref, bf16[2,576,2304]{2,1,0:T(8,128)(2,1)} %get-tuple-element.10.hi_ref, bf16[2,576,2304]{2,1,0:T(8,128)(2,1)} %get-tuple-element.11.mid_ref, bf16[2,576,2304]{2,1,0:T(8,128)(2,1)} %get-tuple-element.12.low_ref), custom_call_target="tpu_custom_call" | custom-call | tf_op jit(solution)/shard_map/pallas_call | solution.py:315
  759.4 7.2 constant_dynamic-slice_fusion.2
  766.7 4.4 pad_maximum_fusion
  (35 shorter events, 24.8 us)
Async XLA Ops:
  7.2 396.8 %all-reduce.2.cloned.1.call-start = ((), (), s32[]{:S(2)}) async-start(), calls=%async_computation | async-start | bytes 7077888 | tf_op jit(solution)/shard_map/psum | solution.py:367
  7.2 5.7 collective-permute-start
  27.3 3.7 slice-start
  31.0 1.6 copy-start.2
  54.1 3.7 slice-start.1
  59.4 8.8 %collective-permute-start.1 = (f32[48,256]{1,0:T(8,128)S(1)}, f32[48,256]{1,0:T(8,128)S(1)}, u32[]{:S(2)}, u32[]{:S(2)}) collective-permute-start(f32[48,256]{1,0:T(8,128)S(1)} %collective-permute-done), channel_id=1, source_target_pairs={{4,0},{8,4},{12,8},{16,12},{20,16},{24,20},{28,24},{32,28},{36,32}... | collective-permute-start | bytes 147464 | tf_op jit(solution)/shard_map/ppermute | solution.py:28
  82.6 3.7 slice-start.2
  87.9 6.1 copy-start
  87.9 6.1 copy-start.1
  96.1 0.8 copy-start.4
  766.7 4.4 copy-start.3
Sparse Core Ops, SparseCore 0:
  96.2 307.7 all-reduce.1

commit v2 on v1

--- a/solution.py
+++ b/solution.py
@@ -1,5 +1,4 @@
 import functools
-import math
 
 import jax
 import jax.numpy as jnp
@@ -17,39 +16,13 @@
 PLANE = 16
 LINE = 8
 COLS = PLANE * ROWS
+LANES = 128
+DAYS = 256
+SPAN = PLANE * DAYS
+LAGS = 12
 
 exact_precision = lax.Precision.HIGHEST
 MESH = pl.DeviceIdType.MESH
-
-
-def passed_along(block, axis, distance):
-    devices = range(lax.axis_size(axis))
-    route = [(i - distance, i) for i in devices if i - distance in devices]
-    return lax.ppermute(block, axis, route)
-
-
-def lag_block(local_rows, extended, first_lag, lag_width):
-    day_count = local_rows.shape[1]
-    span = day_count + lag_width - 1
-    segment = extended[:, first_lag : first_lag + span]
-    repeated = jnp.tile(segment, (1, lag_width + 1))[:, : lag_width * (span + 1)]
-    windows = repeated.reshape(segment.shape[0], lag_width, span + 1)[:, :, :day_count]
-    return jnp.einsum(
-        "lt,mjt->ljm",
-        local_rows,
-        windows,
-        precision=exact_precision,
-        preferred_element_type=jnp.float32,
-    )
-
-
-def lag_products(local_rows, extended):
-    lag_width = math.gcd(M, 128)
-    parts_list = [
-        lag_block(local_rows, extended, first_lag, lag_width)
-        for first_lag in range(0, M, lag_width)
-    ]
-    return jnp.concatenate(parts_list, axis=1)
 
 
 def split3(x):
@@ -60,32 +33,242 @@
     return hi, mid, low
 
 
-def assemble_kernel(window_ref, hi_ref, mid_ref, low_ref):
-    for offset in range(12):
+def peers(plane, low_z, panel):
+    def plane_peer(step):
+        spot_x = (plane // 4 + step // 4) % 4
+        spot_y = (plane % 4 + step % 4) % 4
+        spot = spot_x * 4 + spot_y
+        return spot, (low_z * PLANE + spot, panel)
+
+    return plane_peer
+
+
+def rolled_window(ref, start, width):
+    first = start // LANES
+    rest = start % LANES
+    lanes = lax.broadcasted_iota(jnp.int32, (L, LANES), 1)
+    pieces = [
+        pltpu.roll(
+            ref[:, pl.ds(pl.multiple_of((first + at) * LANES, LANES), LANES)],
+            (LANES - rest) % LANES,
+            1,
+        )
+        for at in range(width // LANES + 1)
+    ]
+    kept = lanes < LANES - rest
+    joined = [jnp.where(kept, pieces[at], pieces[at + 1]) for at in range(width // LANES)]
+    return jnp.concatenate(joined, axis=1)
+
+
+def lag_kernel(
+    series_ref,
+    out_ref,
+    flat,
+    shifted,
+    own,
+    win_hi,
+    win_mid,
+    win_low,
+    mine,
+    theirs,
+    send_s,
+    recv_s,
+    send_c,
+    recv_c,
+    send_f,
+    recv_f,
+    send_h,
+    recv_h,
+):
+    tm = lax.axis_index("tm")
+    panel = lax.axis_index("panel")
+    low_z = tm // PLANE
+    plane = tm % PLANE
+    core = panel % 2
+    group = plane * 2 + core
+    plane_peer = peers(plane, low_z, panel)
+    across = ((1 - low_z) * PLANE + plane, panel)
+    beside = (tm, panel + 1 - 2 * core)
+
+    barrier = pltpu.get_barrier_semaphore()
+    for step in range(1, PLANE):
+        pl.semaphore_signal(barrier, inc=1, device_id=plane_peer(step)[1], device_id_type=MESH)
+    pl.semaphore_signal(barrier, inc=1, device_id=across, device_id_type=MESH)
+    pl.semaphore_signal(barrier, inc=1, device_id=beside, device_id_type=MESH)
+    pl.semaphore_wait(barrier, PLANE + 1)
+
+    def remote(source, target, send, receive, device):
+        return pltpu.make_async_remote_copy(
+            src_ref=source,
+            dst_ref=target,
+            send_sem=send,
+            recv_sem=receive,
+            device_id=device,
+            device_id_type=MESH,
+        )
+
+    place = pl.ds(pl.multiple_of(plane * DAYS, DAYS), DAYS)
+    days = [
+        remote(series_ref, flat.at[:, place], send_s.at[step], recv_s.at[step], plane_peer(step)[1])
+        for step in range(1, PLANE)
+    ]
+    for copy in days:
+        copy.start()
+    flat[:, place] = series_ref[...]
+    for copy in days:
+        copy.wait()
+    halo = remote(
+        flat.at[:, : 2 * DAYS], flat.at[:, SPAN : SPAN + 2 * DAYS], send_h.at[0], recv_h.at[0], across
+    )
+    halo.start()
+    hi, mid, low = split3(flat[:, :SPAN])
+    own[:L] = hi
+    own[L : 2 * L] = mid
+    own[2 * L :] = low
+    halo.wait()
+    beyond = flat[:, SPAN : SPAN + 2 * DAYS]
+    flat[:, SPAN : SPAN + 2 * DAYS] = jnp.where(low_z == 1, jnp.zeros_like(beyond), beyond)
+    shifted[...] = rolled_window(flat, group * LAGS, SPAN + LANES)
+    for lag in range(LAGS):
+        hi, mid, low = split3(shifted[:, lag : lag + SPAN])
+        at = slice(L * lag, L * lag + L)
+        win_hi[at, :] = hi
+        win_mid[at, :] = mid
+        win_low[at, :] = low
+
+    def product(left, right):
+        return lax.dot_general(
+            left, right, (((1,), (1,)), ((), ())), preferred_element_type=jnp.float32
+        )
+
+    first = product(win_hi[...], own[...])
+    second = product(win_mid[...], own[: 2 * L])
+    third = product(win_low[...], own[:L])
+    low_part = first[:, 2 * L :] + second[:, L:] + third
+    sums = first[:, :L] + (first[:, L : 2 * L] + second[:, :L] + low_part)
+    mine[...] = jnp.transpose(sums)
+    half = remote(mine, theirs, send_h.at[1], recv_h.at[1], across)
+    half.start()
+    lanes = lax.broadcasted_iota(jnp.int32, (L, LAGS * L), 1)
+    lag_at = jnp.zeros_like(lanes)
+    for lag in range(1, LAGS):
+        lag_at = lag_at + jnp.where(lanes >= lag * L, 1, 0)
+    counts = (2 * SPAN - (group * LAGS + lag_at)).astype(jnp.float32)
+    half.wait()
+    out_ref[group] = (mine[...] + theirs[...]) / counts
+    sends = [
+        remote(
+            out_ref.at[group], out_ref.at[group], send_c.at[step], recv_c.at[step], plane_peer(step)[1]
+        )
+        for step in range(1, PLANE)
+    ]
+    for copy in sends:
+        copy.start()
+    passed = [remote(out_ref.at[group], out_ref.at[group], send_f.at[0], recv_f.at[0], beside)]
+    passed[0].start()
+    for step in range(1, PLANE):
+        sends[step - 1].wait_recv()
+        spot_x = (plane // 4 + 4 - step // 4) % 4
+        spot_y = (plane % 4 + 4 - step % 4) % 4
+        slot = (spot_x * 4 + spot_y) * 2 + core
+        copy = remote(out_ref.at[slot], out_ref.at[slot], send_f.at[step], recv_f.at[step], beside)
+        copy.start()
+        passed.append(copy)
+    for copy in sends:
+        copy.wait_send()
+    for copy in passed:
+        copy.wait()
+
+
+def lag_blocks(series):
+    vmem = pl.BlockSpec(memory_space=pltpu.VMEM)
+    dma = pltpu.SemaphoreType.DMA
+    return pl.pallas_call(
+        lag_kernel,
+        out_shape=jax.ShapeDtypeStruct((2 * PLANE, L, LAGS * L), jnp.float32),
+        in_specs=[vmem],
+        out_specs=vmem,
+        scratch_shapes=[
+            pltpu.VMEM((L, SPAN + 2 * DAYS), jnp.float32),
+            pltpu.VMEM((L, SPAN + LANES), jnp.float32),
+            pltpu.VMEM((3 * L, SPAN), jnp.bfloat16),
+            pltpu.VMEM((LAGS * L, SPAN), jnp.bfloat16),
+            pltpu.VMEM((LAGS * L, SPAN), jnp.bfloat16),
+            pltpu.VMEM((LAGS * L, SPAN), jnp.bfloat16),
+            pltpu.VMEM((L, LAGS * L), jnp.float32),
+            pltpu.VMEM((L, LAGS * L), jnp.float32),
+            dma((PLANE,)),
+            dma((PLANE,)),
+            dma((PLANE,)),
+            dma((PLANE,)),
+            dma((PLANE,)),
+            dma((PLANE,)),
+            dma((2,)),
+            dma((2,)),
+        ],
+        compiler_params=pltpu.CompilerParams(
+            collective_id=1, has_side_effects=True, vmem_limit_bytes=60 * 1024 * 1024
+        ),
+    )(series)
+
+
+def assemble_kernel(blocks_ref, cov_ref, hi_ref, mid_ref, low_ref, line):
+    tm = lax.axis_index("tm")
+    panel = lax.axis_index("panel")
+    low_z = tm // PLANE
+    plane = tm % PLANE
+    step = pl.program_id(0)
+    pair = 2 * LAGS * L
+
+    @pl.when(step == 0)
+    def _():
+        def lay(at, carry):
+            both = jnp.concatenate([blocks_ref[2 * at], blocks_ref[2 * at + 1]], axis=1)
+            line[:, pl.ds(pl.multiple_of(M * L + at * pair, LANES), pair)] = both
+            after = blocks_ref[jnp.minimum(2 * at + 2, 2 * PLANE - 1)][:, :LANES]
+            turned = jnp.transpose(jnp.concatenate([both, after], axis=1))
+            reversed_blocks = [
+                turned[L * lag : L * lag + L, :] for lag in range(2 * LAGS, 0, -1)
+            ]
+            line[:, pl.ds(pl.multiple_of((PLANE - 1 - at) * pair, LANES), pair)] = jnp.concatenate(
+                reversed_blocks, axis=1
+            )
+            return carry
+
+        lax.fori_loop(0, PLANE, lay, 0)
+
+    own_lag = 3 * (tm * 4 + panel)
+    for offset in range(3):
+        start = L * (M - own_lag - offset) + step * COLS
+        cov_ref[L * offset : L * offset + L, :] = rolled_window(line, start, COLS)
+    h = step // 4
+    spot = step % 4
+    base = L * (372 + (low_z - h) * 192 - 12 * plane + 3 * panel + 12 - 3 * spot - 2)
+    window = rolled_window(line, base, 71 * LANES)
+    for offset in range(3):
         pieces = [
-            window_ref[0, :, L * (11 - offset + 12 * plane) : L * (11 - offset + 12 * plane) + ROWS]
-            for plane in range(PLANE)
+            window[:, L * (2 - offset + 12 * at) : L * (2 - offset + 12 * at) + ROWS]
+            for at in range(PLANE)
         ]
-        rows = jnp.concatenate(pieces, axis=1)
-        hi, mid, low = split3(rows)
+        hi, mid, low = split3(jnp.concatenate(pieces, axis=1))
         at = slice(L * offset, L * offset + L)
         hi_ref[0, at, :] = hi
         mid_ref[0, at, :] = mid
         low_ref[0, at, :] = low
 
 
-def assemble(windows):
-    width = windows.shape[2]
-    shape = jax.ShapeDtypeStruct((2, 12 * L, COLS), jnp.bfloat16)
-    spec = pl.BlockSpec((1, 12 * L, COLS), lambda h: (h, 0, 0))
+def assemble(blocks):
+    shape = jax.ShapeDtypeStruct((LINE, ROWS, COLS), jnp.bfloat16)
+    spec = pl.BlockSpec((1, ROWS, COLS), lambda h: (h, 0, 0))
     return pl.pallas_call(
         assemble_kernel,
-        grid=(2,),
-        out_shape=(shape, shape, shape),
-        in_specs=[pl.BlockSpec((1, L, width), lambda h: (h, 0, 0))],
-        out_specs=(spec, spec, spec),
+        grid=(LINE,),
+        out_shape=(jax.ShapeDtypeStruct((ROWS, M * L), jnp.float32), shape, shape, shape),
+        in_specs=[pl.BlockSpec((2 * PLANE, L, LAGS * L), lambda h: (0, 0, 0))],
+        out_specs=(pl.BlockSpec((ROWS, COLS), lambda h: (0, h)), spec, spec, spec),
+        scratch_shapes=[pltpu.VMEM((L, 2 * M * L + 2 * LANES), jnp.float32)],
         compiler_params=pltpu.CompilerParams(vmem_limit_bytes=60 * 1024 * 1024),
-    )(windows)
+    )(blocks)
 
 
 def exact_dot(left, right, contract):
@@ -353,46 +536,9 @@
 
 
 def local(series, start_block):
-    channels, day_count = series.shape
-    tm_size = lax.axis_size("tm")
-    panel_size = lax.axis_size("panel")
-    total_days = day_count * tm_size
-    reach_hops = (M - 1 + day_count - 1) // day_count
-    pieces = [series]
-    moving = series
-    for distance in range(reach_hops):
-        moving = passed_along(moving, "tm", -1)
-        pieces.append(moving)
-    extended = jnp.concatenate(pieces, axis=1)
-    summed = lax.psum(lag_products(series, extended), "tm")
-    counts = (total_days - jnp.arange(M)).astype(jnp.float32)
-    normed = summed / counts[None, :, None]
-    two_sided = jnp.concatenate([jnp.transpose(normed, (2, 1, 0))[:, :0:-1, :], normed], axis=1)
-    flat = two_sided.reshape(channels, (2 * M - 1) * channels)
-    tm = lax.axis_index("tm")
-    panel = lax.axis_index("panel")
-    block_index = tm * panel_size + panel
-    covariance = jnp.concatenate(
-        [
-            lax.dynamic_slice(
-                flat, (0, (M - 1 - 3 * block_index - offset) * channels), (channels, M * channels)
-            )
-            for offset in range(3)
-        ],
-        axis=0,
-    )
-    windows = jnp.stack(
-        [
-            lax.dynamic_slice(
-                flat,
-                (0, (372 + (tm // PLANE - h) * 192 - 12 * (tm % PLANE) + 3 * panel) * channels),
-                (channels, 194 * channels),
-            )
-            for h in range(2)
-        ]
-    )
-    hi, mid, low = assemble(windows)
-    basis, diag, off = lanczos(start_block, hi, mid, low)
+    covariance, hi, mid, low = assemble(lag_blocks(series))
+    shape = (2, 12 * L, COLS)
+    basis, diag, off = lanczos(start_block, hi.reshape(shape), mid.reshape(shape), low.reshape(shape))
     return covariance, basis, diag[1:], off
 
 

time: 793 us -> 353 us (0.45); the launches traced: 779 us -> 352 us
  waiting for transfers between devices: 310 us -> 0 us
  local copies, waits for them, and re-layouts: 123 us -> 6.08 us
  Pallas kernels: 293 us -> 346 us
  matrix products: 20.3 us -> 0 us
  other arithmetic: 15.2 us -> 0 us
  between operations: 14.4 us -> 0.66 us
    psum x1 -> x0, waiting for transfers between devices: 306 us -> none  [local(): summed = lax.psum(lag_products(series, extended), 'tm')]
    pallas_call x1 -> x2, Pallas kernels: 9.31 us -> 82.2 us  [the longest x1 60 us: lag_blocks(): pl.pallas_call(lag_kernel, out_shape=jax.ShapeDtypeStruct((2 * PLANE, L,...]
    another operation x7 -> x0, local copies, waits for them, and re-layouts: 46.2 us -> none  [the longest x6 43.1 us: lag_block(): repeated = jnp.tile(segment, (1, lag_width + 1))[:, :lag_width * (span + 1)]]
    dot_general x3 -> x0, matrix products: 20.3 us -> none  [lag_block(): jnp.einsum('lt,mjt->ljm', local_rows, windows, precision=exact_precision,...]
    pallas_call x1, Pallas kernels: 283 us -> 264 us  [lanczos(): pl.pallas_call(lanczos_kernel, out_shape=(jax.ShapeDtypeStruct((ITERS + 1...]
    reshape x1 -> x0, local copies, waits for them, and re-layouts: 19.5 us -> none  [local(): flat = two_sided.reshape(channels, (2 * M - 1) * channels)]
    unnamed x19 -> x5, local copies, waits for them, and re-layouts: 20.6 us -> 4.47 us
    slice x8 -> x0, local copies, waits for them, and re-layouts: 13.8 us -> none  [the longest x6 11 us: lag_block(): repeated = jnp.tile(segment, (1, lag_width + 1))[:, :lag_width * (span + 1)]]
  transfers between devices with their start and end apart: 3 -> 0, of which waited for: 2 -> 0; matrix products, arithmetic and copies ran while one was open for 1% -> 0% of each run, Pallas kernels for 0% -> 0%
where the time goes in v2:
time: 353 us; the launch traced here: 352 us
  Pallas kernels  346 us (98%)
  local copies, waits for them, and re-layouts  6.08 us (2%)
    pallas_call x1, Pallas kernels, lanczos(): pl.pallas_call(lanczos_kernel, out_shape=(jax.ShapeDtypeStruct((ITERS + 1...  264 us
    pallas_call x1, Pallas kernels, lag_blocks(): pl.pallas_call(lag_kernel, out_shape=jax.ShapeDtypeStruct((2 * PLANE, L,...  60 us
    pallas_call x1, Pallas kernels, assemble(): pl.pallas_call(assemble_kernel, grid=(LINE,), out_shape=(jax.ShapeDtypeSt...  22.2 us

profile of v2, /device:TPU:1, one launch (start us, length us, event | category | flops | bytes accessed | tf_op | source)
XLA Modules:
  0.0 352.5 jit_solution(10952616021699085438)
XLA Ops:
  0.6 0.0 copy-start
  0.6 60.0 %shard_map.57.blocks_ref = f32[32,48,576]{2,1,0:T(8,128)} custom-call(f32[48,256]{1,0:T(8,128)} %series_ref.1), custom_call_target="tpu_custom_call" | custom-call | tf_op jit(solution)/shard_map/pallas_call | solution.py:186
  60.6 22.2 %shard_map.58 = (f32[144,18432]{1,0:T(8,128)}, bf16[8,144,2304]{2,1,0:T(8,128)(2,1)}, bf16[8,144,2304]{2,1,0:T(8,128)(2,1)}, bf16[8,144,2304]{2,1,0:T(8,128)(2,1)}) custom-call(f32[32,48,576]{2,1,0:T(8,128)} %shard_map.57.blocks_ref), custom_call_target="tpu_custom_call" | custom-call | tf_op jit(solution)/shard_map/pallas_call | solution.py:263
  82.8 0.0 copy-done
  82.8 0.7 copy.6.start_ref
  83.5 263.6 %shard_map.59 = (f32[7,144,64]{2,1,0:T(8,128)}, f32[7,64,64]{2,1,0:T(8,128)}, f32[7,64,64]{2,1,0:T(8,128)}) custom-call(f32[144,64]{1,0:T(8,128)} %copy.6.start_ref, bf16[2,576,2304]{2,1,0:T(8,128)(2,1)} %bitcast.3, bf16[2,576,2304]{2,1,0:T(8,128)(2,1)} %bitcast.4, bf16[2,576,2304]{2,1,0:T(8,128)(2,1)} %bitcast.5), custom_call_target="tpu_custom_call" | custom-call | tf_op jit(solution)/shard_map/pallas_call | solution.py:498
  347.1 2.1 copy.7
  349.2 1.6 slice.3
  350.9 1.6 copy.9
Async XLA Ops:
  0.6 82.2 %copy-start = (f32[144,64]{0,1:T(8,128)S(1)}, f32[144,64]{0,1:T(8,128)}, u32[]{:S(2)}) copy-start(f32[144,64]{0,1:T(8,128)} %param.3) | copy-start | bytes 110596

commit v3 on v2

--- a/solution.py
+++ b/solution.py
@@ -308,6 +308,21 @@
     return upper, inverse
 
 
+def hops(step):
+    return (0, 1, 2, 1)[step // 4] + (0, 1, 2, 1)[step % 4]
+
+
+FAR_FIRST = sorted(range(1, PLANE), key=lambda step: -hops(step))
+
+
+def pack(block):
+    return jnp.concatenate([block[:HALF], block[HALF:]], axis=1)
+
+
+def unpack(block):
+    return jnp.concatenate([block[:, :B], block[:, B:]], axis=0)
+
+
 def lanczos_kernel(
     start_ref,
     hi_ref,
@@ -316,8 +331,12 @@
     basis_ref,
     diag_ref,
     off_ref,
+    tile_hi,
+    tile_mid,
+    tile_low,
     work,
     current,
+    applied,
     packed,
     gathered,
     stacked,
@@ -329,6 +348,7 @@
     stage2,
     total,
     full,
+    tile_sem,
     send_q,
     recv_q,
     send_p,
@@ -345,12 +365,16 @@
     low_z = tm // PLANE
     plane = tm % PLANE
     line = low_z * 4 + panel
-
-    def plane_peer(step):
-        spot_x = (plane // 4 + step // 4) % 4
-        spot_y = (plane % 4 + step % 4) % 4
-        spot = spot_x * 4 + spot_y
-        return spot, (low_z * PLANE + spot, panel)
+    tiles = [
+        pltpu.make_async_copy(source, target, tile_sem.at[at])
+        for at, (source, target) in enumerate(
+            ((hi_ref, tile_hi), (mid_ref, tile_mid), (low_ref, tile_low))
+        )
+    ]
+    for copy in tiles:
+        copy.start()
+
+    plane_peer = peers(plane, low_z, panel)
 
     def line_peer(step):
         spot_z = (low_z + step // 4) % 2
@@ -364,168 +388,217 @@
         pl.semaphore_signal(barrier, inc=1, device_id=line_peer(step)[1], device_id_type=MESH)
     pl.semaphore_wait(barrier, PLANE + LINE - 2)
 
-    def plane_copy(step, source, target, sends, receives):
-        spot, device = plane_peer(step)
+    def remote(source, target, send, receive, device):
         return pltpu.make_async_remote_copy(
             src_ref=source,
-            dst_ref=target.at[plane],
-            send_sem=sends.at[step],
-            recv_sem=receives.at[step],
+            dst_ref=target,
+            send_sem=send,
+            recv_sem=receive,
             device_id=device,
             device_id_type=MESH,
         )
 
-    def line_copy(step, source, target, sends, receives):
-        return pltpu.make_async_remote_copy(
-            src_ref=source,
-            dst_ref=target,
-            send_sem=sends.at[step],
-            recv_sem=receives.at[step],
-            device_id=line_peer(step)[1],
-            device_id_type=MESH,
-        )
-
-    def gram_total(basis_block, rows_block):
-        both = jnp.concatenate([basis_block, rows_block], axis=1)
+    work[...] = start_ref[...]
+    current[...] = jnp.zeros_like(current)
+    applied[...] = jnp.zeros_like(applied)
+
+    def one_step(step_at, last):
+        slot = step_at % 2
+        before = current[...]
+        rows_block = work[...]
+        blocks = [
+            remote(
+                packed,
+                gathered.at[slot, plane],
+                send_q.at[step],
+                recv_q.at[slot, step],
+                plane_peer(step)[1],
+            )
+            for step in FAR_FIRST
+            if not last
+        ]
+        if not last:
+            packed[...] = pack(rows_block)
+            for copy in blocks:
+                copy.start()
+
+        both = jnp.concatenate([before, rows_block], axis=1)
         gram[...] = exact_dot(both, both, ((0,), (0,))).reshape(LINE, 16, 2 * B)
         firsts = [
-            line_copy(step, gram.at[line_peer(step)[0]], stage1.at[line], send_1, recv_1)
+            remote(
+                gram.at[line_peer(step)[0]],
+                stage1.at[line],
+                send_1.at[step],
+                recv_1.at[step],
+                line_peer(step)[1],
+            )
             for step in range(1, LINE)
         ]
         for copy in firsts:
             copy.start()
         stage1[line] = gram[line]
+
+        def lay(spot, block):
+            hi, mid, low = split3(unpack(block))
+            at = pl.ds(pl.multiple_of(spot * ROWS, ROWS), ROWS)
+            stacked[at, :] = jnp.concatenate([hi, mid, low], axis=1)
+
+        if not last:
+            lay(plane, packed[...])
         for copy in firsts:
             copy.wait()
         reduced = stage1[0]
         for spot in range(1, LINE):
             reduced = reduced + stage1[spot]
         slab[...] = reduced
-        stage2[plane] = reduced
-        seconds = [plane_copy(step, slab, stage2, send_2, recv_2) for step in range(1, PLANE)]
+        stage2[slot, plane] = reduced
+        seconds = [
+            remote(
+                slab,
+                stage2.at[slot, plane],
+                send_2.at[step],
+                recv_2.at[slot, step],
+                plane_peer(step)[1],
+            )
+            for step in FAR_FIRST
+        ]
         for copy in seconds:
             copy.start()
+
+        sums = [
+            remote(
+                partial.at[line_peer(step)[0]],
+                landed.at[slot, line],
+                send_p.at[step],
+                recv_p.at[slot, step],
+                line_peer(step)[1],
+            )
+            for step in range(1, LINE)
+            if not last
+        ]
+
+        def multiply(h, carry):
+            first = jnp.dot(tile_hi[h], stacked[...], preferred_element_type=jnp.float32)
+            second = jnp.dot(
+                tile_mid[h], stacked[:, : 2 * B], preferred_element_type=jnp.float32
+            )
+            third = jnp.dot(tile_low[h], stacked[:, :B], preferred_element_type=jnp.float32)
+            low_part = third + second[:, B:] + first[:, 2 * B :]
+            product = first[:, :B] + (first[:, B : 2 * B] + second[:, :B] + low_part)
+            for spot in range(4):
+                rows = product[spot * ROWS : (spot + 1) * ROWS]
+                partial[h * 4 + spot] = pack(rows)
+            return carry
+
+        if not last:
+            for copy, step in zip(blocks, FAR_FIRST):
+                copy.wait()
+                spot_x = (plane // 4 + 4 - step // 4) % 4
+                spot_y = (plane % 4 + 4 - step % 4) % 4
+                spot = spot_x * 4 + spot_y
+                lay(spot, gathered[slot, spot])
+
+            @pl.when(step_at == 0)
+            def _():
+                for copy in tiles:
+                    copy.wait()
+
+            lax.fori_loop(0, 2, multiply, 0)
+            for copy in sums:
+                copy.start()
+            landed[slot, line] = partial[line]
+
         for copy in seconds:
             copy.wait()
-        reduced = stage2[0]
+        reduced = stage2[slot, 0]
         for spot in range(1, PLANE):
-            reduced = reduced + stage2[spot]
+            reduced = reduced + stage2[slot, spot]
         total[...] = reduced
         full[line] = reduced
-        thirds = [line_copy(step, total, full.at[line], send_3, recv_3) for step in range(1, LINE)]
+        thirds = [
+            remote(total, full.at[line], send_3.at[step], recv_3.at[step], line_peer(step)[1])
+            for step in range(1, LINE)
+        ]
         for copy in thirds:
             copy.start()
         for copy in thirds:
             copy.wait()
-        return full[...].reshape(2 * B, 2 * B)
-
-    work[...] = start_ref[...]
-    current[...] = jnp.zeros_like(current)
-
-    def one_step(step_at, carry):
-        summed = gram_total(current[...], work[...])
+        summed = full[...].reshape(2 * B, 2 * B)
         basis_gram = summed[:B, :B]
         diagonal = summed[:B, B:]
         work_gram = summed[B:, B:]
         weighted = exact_dot(basis_gram, diagonal, ((1,), (0,)))
         left = exact_dot(diagonal, 2.0 * diagonal - weighted, ((0,), (0,)))
         upper, inverse = factor(work_gram - left)
-        reduced = work[...] - exact_dot(current[...], diagonal, ((1,), (0,)))
+        diag_ref[jnp.maximum(step_at - 1, 0)] = diagonal
+        off_ref[step_at] = upper
+        if last:
+            reduced = rows_block - exact_dot(before, diagonal, ((1,), (0,)))
+            basis_ref[step_at] = exact_dot(reduced, inverse, ((1,), (1,)))
+            return
+        for copy in sums:
+            copy.wait()
+        value = landed[slot, 0]
+        for spot in range(1, LINE):
+            value = value + landed[slot, spot]
+        old = jnp.concatenate([before, applied[...]], axis=0)
+        new = jnp.concatenate([rows_block, unpack(value)], axis=0)
+        reduced = new - exact_dot(old, diagonal, ((1,), (0,)))
         fresh = exact_dot(reduced, inverse, ((1,), (1,)))
-        diag_ref[step_at] = diagonal
-        off_ref[step_at] = upper
-        basis_ref[step_at] = fresh
-
-        @pl.when(step_at < ITERS)
-        def _():
-            block = jnp.concatenate([fresh[:HALF], fresh[HALF:]], axis=1)
-            packed[...] = block
-            gathered[plane] = block
-            copies = [plane_copy(step, packed, gathered, send_q, recv_q) for step in range(1, PLANE)]
-            for copy in copies:
-                copy.start()
-            back = exact_dot(current[...], upper, ((1,), (1,)))
-            current[...] = fresh
-            for copy in copies:
-                copy.wait()
-
-            def unpack(spot, carry):
-                block = gathered[spot]
-                block = jnp.concatenate([block[:, :B], block[:, B:]], axis=0)
-                hi, mid, low = split3(block)
-                at = pl.ds(pl.multiple_of(spot * ROWS, ROWS), ROWS)
-                stacked[at, :] = jnp.concatenate([hi, mid, low], axis=1)
-                return carry
-
-            lax.fori_loop(0, PLANE, unpack, 0)
-
-            def multiply(h, carry):
-                first = jnp.dot(hi_ref[h], stacked[...], preferred_element_type=jnp.float32)
-                second = jnp.dot(
-                    mid_ref[h], stacked[:, : 2 * B], preferred_element_type=jnp.float32
-                )
-                third = jnp.dot(low_ref[h], stacked[:, :B], preferred_element_type=jnp.float32)
-                low_part = third + second[:, B:] + first[:, 2 * B :]
-                product = first[:, :B] + (first[:, B : 2 * B] + second[:, :B] + low_part)
-                for spot in range(4):
-                    rows = product[spot * ROWS : (spot + 1) * ROWS]
-                    partial[h * 4 + spot] = jnp.concatenate([rows[:HALF], rows[HALF:]], axis=1)
-                return carry
-
-            lax.fori_loop(0, 2, multiply, 0)
-            sums = [
-                line_copy(step, partial.at[line_peer(step)[0]], landed.at[line], send_p, recv_p)
-                for step in range(1, LINE)
-            ]
-            for copy in sums:
-                copy.start()
-            landed[line] = partial[line]
-            for copy in sums:
-                copy.wait()
-            value = landed[0]
-            for spot in range(1, LINE):
-                value = value + landed[spot]
-            work[...] = jnp.concatenate([value[:, :B], value[:, B:]], axis=0) - back
-
+        basis_ref[step_at] = fresh[:ROWS]
+        current[...] = fresh[:ROWS]
+        applied[...] = fresh[ROWS:]
+        work[...] = fresh[ROWS:] - exact_dot(before, upper, ((1,), (1,)))
+
+    def body(step_at, carry):
+        one_step(step_at, False)
         return carry
 
-    lax.fori_loop(0, ITERS + 1, one_step, 0)
+    lax.fori_loop(0, ITERS, body, 0)
+    one_step(ITERS, True)
 
 
 def lanczos(start, hi, mid, low):
     vmem = pl.BlockSpec(memory_space=pltpu.VMEM)
+    away = pl.BlockSpec(memory_space=pl.ANY)
     dma = pltpu.SemaphoreType.DMA
+    tile = pltpu.VMEM((2, 4 * ROWS, COLS), jnp.bfloat16)
     return pl.pallas_call(
         lanczos_kernel,
         out_shape=(
             jax.ShapeDtypeStruct((ITERS + 1, ROWS, B), jnp.float32),
-            jax.ShapeDtypeStruct((ITERS + 1, B, B), jnp.float32),
+            jax.ShapeDtypeStruct((ITERS, B, B), jnp.float32),
             jax.ShapeDtypeStruct((ITERS + 1, B, B), jnp.float32),
         ),
-        in_specs=[vmem] * 4,
+        in_specs=[vmem, away, away, away],
         out_specs=(vmem, vmem, vmem),
         scratch_shapes=[
+            tile,
+            tile,
+            tile,
+            pltpu.VMEM((ROWS, B), jnp.float32),
             pltpu.VMEM((ROWS, B), jnp.float32),
             pltpu.VMEM((ROWS, B), jnp.float32),
             pltpu.VMEM((HALF, 2 * B), jnp.float32),
-            pltpu.VMEM((PLANE, HALF, 2 * B), jnp.float32),
+            pltpu.VMEM((2, PLANE, HALF, 2 * B), jnp.float32),
             pltpu.VMEM((COLS, 3 * B), jnp.bfloat16),
             pltpu.VMEM((LINE, HALF, 2 * B), jnp.float32),
-            pltpu.VMEM((LINE, HALF, 2 * B), jnp.float32),
+            pltpu.VMEM((2, LINE, HALF, 2 * B), jnp.float32),
             pltpu.VMEM((LINE, 16, 2 * B), jnp.float32),
             pltpu.VMEM((LINE, 16, 2 * B), jnp.float32),
             pltpu.VMEM((16, 2 * B), jnp.float32),
-            pltpu.VMEM((PLANE, 16, 2 * B), jnp.float32),
+            pltpu.VMEM((2, PLANE, 16, 2 * B), jnp.float32),
             pltpu.VMEM((16, 2 * B), jnp.float32),
             pltpu.VMEM((LINE, 16, 2 * B), jnp.float32),
-            dma((PLANE,)),
-            dma((PLANE,)),
+            dma((3,)),
+            dma((PLANE,)),
+            dma((2, PLANE)),
+            dma((LINE,)),
+            dma((2, LINE)),
             dma((LINE,)),
             dma((LINE,)),
-            dma((LINE,)),
-            dma((LINE,)),
-            dma((PLANE,)),
-            dma((PLANE,)),
+            dma((PLANE,)),
+            dma((2, PLANE)),
             dma((LINE,)),
             dma((LINE,)),
         ],
@@ -539,7 +612,7 @@
     covariance, hi, mid, low = assemble(lag_blocks(series))
     shape = (2, 12 * L, COLS)
     basis, diag, off = lanczos(start_block, hi.reshape(shape), mid.reshape(shape), low.reshape(shape))
-    return covariance, basis, diag[1:], off
+    return covariance, basis, diag, off
 
 
 def solution(mesh):

time: 353 us -> 267 us (0.76)
  Pallas kernels: 346 us -> 260 us
    pallas_call x1, Pallas kernels: 264 us -> 178 us  [lanczos(): pl.pallas_call(lanczos_kernel, out_shape=(jax.ShapeDtypeStruct((ITERS + 1...]
where the time goes in v3:
time: 267 us
  Pallas kernels  260 us (97%)
  local copies, waits for them, and re-layouts  6.08 us (2%)
    pallas_call x1, Pallas kernels, lanczos(): pl.pallas_call(lanczos_kernel, out_shape=(jax.ShapeDtypeStruct((ITERS + 1...  178 us
    pallas_call x1, Pallas kernels, lag_blocks(): pl.pallas_call(lag_kernel, out_shape=jax.ShapeDtypeStruct((2 * PLANE, L,...  60 us
    pallas_call x1, Pallas kernels, assemble(): pl.pallas_call(assemble_kernel, grid=(LINE,), out_shape=(jax.ShapeDtypeSt...  22.4 us
    unnamed x6, local copies, waits for them, and re-layouts  6.08 us

profile of v3, /device:TPU:1, one launch (start us, length us, event | category | flops | bytes accessed | tf_op | source)
XLA Modules:
  0.0 266.9 jit_solution(15674340410422318733)
XLA Ops:
  0.6 0.0 copy-start
  0.6 60.0 %shard_map.57.blocks_ref = f32[32,48,576]{2,1,0:T(8,128)} custom-call(f32[48,256]{1,0:T(8,128)} %series_ref.1), custom_call_target="tpu_custom_call" | custom-call | tf_op jit(solution)/shard_map/pallas_call | solution.py:186
  60.6 22.4 %shard_map.58 = (f32[144,18432]{1,0:T(8,128)}, bf16[8,144,2304]{2,1,0:T(8,128)(2,1)}, bf16[8,144,2304]{2,1,0:T(8,128)(2,1)}, bf16[8,144,2304]{2,1,0:T(8,128)(2,1)}) custom-call(f32[32,48,576]{2,1,0:T(8,128)} %shard_map.57.blocks_ref), custom_call_target="tpu_custom_call" | custom-call | tf_op jit(solution)/shard_map/pallas_call | solution.py:263
  83.0 0.0 copy-done
  83.0 0.7 copy.6.start_ref
  83.7 177.8 %shard_map.59 = (f32[7,144,64]{2,1,0:T(8,128)}, f32[6,64,64]{2,1,0:T(8,128)}, f32[7,64,64]{2,1,0:T(8,128)}) custom-call(f32[144,64]{1,0:T(8,128)} %copy.6.start_ref, bf16[2,576,2304]{2,1,0:T(8,128)(2,1)} %bitcast.3, bf16[2,576,2304]{2,1,0:T(8,128)(2,1)} %bitcast.4, bf16[2,576,2304]{2,1,0:T(8,128)(2,1)} %bitcast.5), custom_call_target="tpu_custom_call" | custom-call | tf_op jit(solution)/shard_map/pallas_call | solution.py:566
  261.5 2.1 copy.7
  263.6 1.6 copy.10
  265.2 1.6 copy.11
Async XLA Ops:
  0.6 82.4 %copy-start = (f32[144,64]{0,1:T(8,128)S(1)}, f32[144,64]{0,1:T(8,128)}, u32[]{:S(2)}) copy-start(f32[144,64]{0,1:T(8,128)} %param.3) | copy-start | bytes 110596

commit v4 on v3

--- a/solution.py
+++ b/solution.py
@@ -16,6 +16,7 @@
 PLANE = 16
 LINE = 8
 COLS = PLANE * ROWS
+HALF_COLS = COLS // 2
 LANES = 128
 DAYS = 256
 SPAN = PLANE * DAYS
@@ -308,11 +309,9 @@
     return upper, inverse
 
 
-def hops(step):
-    return (0, 1, 2, 1)[step // 4] + (0, 1, 2, 1)[step % 4]
-
-
-FAR_FIRST = sorted(range(1, PLANE), key=lambda step: -hops(step))
+PAIR_FIRST = [(0, y) for y in (2, 1, 3)] + [(1, y) for y in (2, 1, 3, 0)]
+PAIR_LAST = [(2, y) for y in (2, 1, 3, 0)] + [(3, y) for y in (2, 1, 3, 0)]
+FAR_FIRST = [10, 6, 14, 9, 11, 2, 8, 5, 7, 13, 15, 1, 3, 4, 12]
 
 
 def pack(block):
@@ -340,6 +339,7 @@
     packed,
     gathered,
     stacked,
+    accumulated,
     partial,
     landed,
     gram,
@@ -381,6 +381,13 @@
         spot_p = (panel + step % 4) % 4
         return spot_z * 4 + spot_p, (spot_z * PLANE + plane, spot_p)
 
+    pair_at = plane // 8
+    odd_x = (plane // 4) % 2
+
+    def x_at(turn):
+        side = (pair_at + turn // 2) % 2
+        return side * 2 + (odd_x + turn) % 2
+
     barrier = pltpu.get_barrier_semaphore()
     for step in range(1, PLANE):
         pl.semaphore_signal(barrier, inc=1, device_id=plane_peer(step)[1], device_id_type=MESH)
@@ -406,20 +413,29 @@
         slot = step_at % 2
         before = current[...]
         rows_block = work[...]
-        blocks = [
-            remote(
-                packed,
-                gathered.at[slot, plane],
-                send_q.at[step],
-                recv_q.at[slot, step],
-                plane_peer(step)[1],
-            )
-            for step in FAR_FIRST
-            if not last
-        ]
+
+        def block_copies(places, first):
+            found = []
+            for at, (turn, y) in enumerate(places):
+                to_x = x_at(turn)
+                to_y = (plane % 4 + y) % 4
+                from_y = (plane % 4 + 4 - y) % 4
+                to_spot = to_x * 4 + to_y
+                copy = remote(
+                    packed,
+                    gathered.at[slot, plane],
+                    send_q.at[first + at],
+                    recv_q.at[slot, first + at],
+                    (low_z * PLANE + to_spot, panel),
+                )
+                found.append((copy, x_at(turn) * 4 + from_y))
+            return found
+
+        near = [] if last else block_copies(PAIR_FIRST, 0)
+        far = [] if last else block_copies(PAIR_LAST, len(PAIR_FIRST))
         if not last:
             packed[...] = pack(rows_block)
-            for copy in blocks:
+            for copy, _ in near + far:
                 copy.start()
 
         both = jnp.concatenate([before, rows_block], axis=1)
@@ -477,25 +493,39 @@
             if not last
         ]
 
-        def multiply(h, carry):
-            first = jnp.dot(tile_hi[h], stacked[...], preferred_element_type=jnp.float32)
+        def multiply(h, half):
+            lanes = pl.ds(pl.multiple_of(half * HALF_COLS, HALF_COLS), HALF_COLS)
+            first = jnp.dot(tile_hi[h, :, lanes], stacked[lanes, :], preferred_element_type=jnp.float32)
             second = jnp.dot(
-                tile_mid[h], stacked[:, : 2 * B], preferred_element_type=jnp.float32
+                tile_mid[h, :, lanes], stacked[lanes, : 2 * B], preferred_element_type=jnp.float32
             )
-            third = jnp.dot(tile_low[h], stacked[:, :B], preferred_element_type=jnp.float32)
+            third = jnp.dot(
+                tile_low[h, :, lanes], stacked[lanes, :B], preferred_element_type=jnp.float32
+            )
             low_part = third + second[:, B:] + first[:, 2 * B :]
-            product = first[:, :B] + (first[:, B : 2 * B] + second[:, :B] + low_part)
+            return first[:, :B] + (first[:, B : 2 * B] + second[:, :B] + low_part)
+
+        def send_sums(h):
+            for at, copy in enumerate(sums):
+                @pl.when((low_z + (at + 1) // 4) % 2 == h)
+                def _():
+                    copy.start()
+
+            @pl.when(low_z == h)
+            def _():
+                landed[slot, line] = partial[line]
+
+        def finish(h):
+            product = accumulated[h] + multiply(h, other)
             for spot in range(4):
                 rows = product[spot * ROWS : (spot + 1) * ROWS]
                 partial[h * 4 + spot] = pack(rows)
-            return carry
-
+            send_sums(h)
+
+        other = 1 - pair_at
         if not last:
-            for copy, step in zip(blocks, FAR_FIRST):
+            for copy, spot in near:
                 copy.wait()
-                spot_x = (plane // 4 + 4 - step // 4) % 4
-                spot_y = (plane % 4 + 4 - step % 4) % 4
-                spot = spot_x * 4 + spot_y
                 lay(spot, gathered[slot, spot])
 
             @pl.when(step_at == 0)
@@ -503,10 +533,15 @@
                 for copy in tiles:
                     copy.wait()
 
-            lax.fori_loop(0, 2, multiply, 0)
-            for copy in sums:
-                copy.start()
-            landed[slot, line] = partial[line]
+            def begin(h, carry):
+                accumulated[h] = multiply(h, pair_at)
+                return carry
+
+            lax.fori_loop(0, 2, begin, 0)
+            for copy, spot in far:
+                copy.wait()
+                lay(spot, gathered[slot, spot])
+            finish(0)
 
         for copy in seconds:
             copy.wait()
@@ -521,6 +556,8 @@
         ]
         for copy in thirds:
             copy.start()
+        if not last:
+            finish(1)
         for copy in thirds:
             copy.wait()
         summed = full[...].reshape(2 * B, 2 * B)
@@ -582,6 +619,7 @@
             pltpu.VMEM((HALF, 2 * B), jnp.float32),
             pltpu.VMEM((2, PLANE, HALF, 2 * B), jnp.float32),
             pltpu.VMEM((COLS, 3 * B), jnp.bfloat16),
+            pltpu.VMEM((2, 4 * ROWS, B), jnp.float32),
             pltpu.VMEM((LINE, HALF, 2 * B), jnp.float32),
             pltpu.VMEM((2, LINE, HALF, 2 * B), jnp.float32),
             pltpu.VMEM((LINE, 16, 2 * B), jnp.float32),

time: 267 us -> 264 us (0.989)
  Pallas kernels: 260 us -> 257 us
    pallas_call x1, Pallas kernels: 178 us -> 175 us  [lanczos(): pl.pallas_call(lanczos_kernel, out_shape=(jax.ShapeDtypeStruct((ITERS + 1...]
where the time goes in v4:
time: 264 us
  Pallas kernels  257 us (97%)
  local copies, waits for them, and re-layouts  6.08 us (2%)
    pallas_call x1, Pallas kernels, lanczos(): pl.pallas_call(lanczos_kernel, out_shape=(jax.ShapeDtypeStruct((ITERS + 1...  175 us
    pallas_call x1, Pallas kernels, lag_blocks(): pl.pallas_call(lag_kernel, out_shape=jax.ShapeDtypeStruct((2 * PLANE, L,...  60 us
    pallas_call x1, Pallas kernels, assemble(): pl.pallas_call(assemble_kernel, grid=(LINE,), out_shape=(jax.ShapeDtypeSt...  22.4 us
    unnamed x6, local copies, waits for them, and re-layouts  6.08 us

profile of v4, /device:TPU:1, one launch (start us, length us, event | category | flops | bytes accessed | tf_op | source)
XLA Modules:
  0.0 263.7 jit_solution(12043275936970614114)
XLA Ops:
  0.6 0.0 copy-start
  0.6 60.0 %shard_map.57.blocks_ref = f32[32,48,576]{2,1,0:T(8,128)} custom-call(f32[48,256]{1,0:T(8,128)} %series_ref.1), custom_call_target="tpu_custom_call" | custom-call | tf_op jit(solution)/shard_map/pallas_call | solution.py:187
  60.6 22.4 %shard_map.58 = (f32[144,18432]{1,0:T(8,128)}, bf16[8,144,2304]{2,1,0:T(8,128)(2,1)}, bf16[8,144,2304]{2,1,0:T(8,128)(2,1)}, bf16[8,144,2304]{2,1,0:T(8,128)(2,1)}) custom-call(f32[32,48,576]{2,1,0:T(8,128)} %shard_map.57.blocks_ref), custom_call_target="tpu_custom_call" | custom-call | tf_op jit(solution)/shard_map/pallas_call | solution.py:264
  83.0 0.0 copy-done
  83.0 0.7 copy.6.start_ref
  83.7 174.6 %shard_map.59 = (f32[7,144,64]{2,1,0:T(8,128)}, f32[6,64,64]{2,1,0:T(8,128)}, f32[7,64,64]{2,1,0:T(8,128)}) custom-call(f32[144,64]{1,0:T(8,128)} %copy.6.start_ref, bf16[2,576,2304]{2,1,0:T(8,128)(2,1)} %bitcast.3, bf16[2,576,2304]{2,1,0:T(8,128)(2,1)} %bitcast.4, bf16[2,576,2304]{2,1,0:T(8,128)(2,1)} %bitcast.5), custom_call_target="tpu_custom_call" | custom-call | tf_op jit(solution)/shard_map/pallas_call | solution.py:603
  258.3 2.1 copy.7
  260.4 1.6 copy.10
  262.1 1.6 copy.11
Async XLA Ops:
  0.6 82.4 %copy-start = (f32[144,64]{0,1:T(8,128)S(1)}, f32[144,64]{0,1:T(8,128)}, u32[]{:S(2)}) copy-start(f32[144,64]{0,1:T(8,128)} %param.3) | copy-start | bytes 110596

commit v5 on v4

--- a/solution.py
+++ b/solution.py
@@ -63,7 +63,8 @@
 
 def lag_kernel(
     series_ref,
-    out_ref,
+    line,
+    blocks,
     flat,
     shifted,
     own,
@@ -74,6 +75,8 @@
     theirs,
     send_s,
     recv_s,
+    send_d,
+    recv_d,
     send_c,
     recv_c,
     send_f,
@@ -108,15 +111,45 @@
             device_id_type=MESH,
         )
 
-    place = pl.ds(pl.multiple_of(plane * DAYS, DAYS), DAYS)
+    x = plane // 4
+    y = plane % 4
+    share = L // 2
+
+    def spot_at(turn_x, turn_y):
+        return ((x + turn_x) % 4) * 4 + (y + turn_y) % 4
+
+    def chip_at(spot):
+        return (low_z * PLANE + spot, panel)
+
+    turns = [(p, q) for p in (2, 1, 3, 0) for q in (2, 1, 3, 0) if p or q]
+    rows = pl.ds(pl.multiple_of(core * share, share), share)
+
+    def place(spot):
+        return pl.ds(pl.multiple_of(spot * DAYS, DAYS), DAYS)
+
+    flat[:, place(plane)] = series_ref[...]
     days = [
-        remote(series_ref, flat.at[:, place], send_s.at[step], recv_s.at[step], plane_peer(step)[1])
-        for step in range(1, PLANE)
+        remote(
+            series_ref.at[rows],
+            flat.at[rows, place(plane)],
+            send_s.at[at],
+            recv_s.at[at],
+            chip_at(spot_at(*turn)),
+        )
+        for at, turn in enumerate(turns)
     ]
     for copy in days:
         copy.start()
-    flat[:, place] = series_ref[...]
+    shared = []
+    for at, turn in enumerate(turns):
+        days[at].wait_recv()
+        held = flat.at[rows, place(spot_at(-turn[0] + 4, -turn[1] + 4))]
+        copy = remote(held, held, send_d.at[at], recv_d.at[at], beside)
+        copy.start()
+        shared.append(copy)
     for copy in days:
+        copy.wait_send()
+    for copy in shared:
         copy.wait()
     halo = remote(
         flat.at[:, : 2 * DAYS], flat.at[:, SPAN : SPAN + 2 * DAYS], send_h.at[0], recv_h.at[0], across
@@ -156,29 +189,99 @@
         lag_at = lag_at + jnp.where(lanes >= lag * L, 1, 0)
     counts = (2 * SPAN - (group * LAGS + lag_at)).astype(jnp.float32)
     half.wait()
-    out_ref[group] = (mine[...] + theirs[...]) / counts
-    sends = [
-        remote(
-            out_ref.at[group], out_ref.at[group], send_c.at[step], recv_c.at[step], plane_peer(step)[1]
+    blocks[group] = (mine[...] + theirs[...]) / counts
+
+    def held(spot, color):
+        return blocks.at[spot * 2 + core, pl.ds(color * share, share)]
+
+    started = []
+
+    def forward(origin_x, origin_y, color, along, to_turn):
+        to_x, to_y = (to_turn, 0) if along == 0 else (0, to_turn)
+        source = held(spot_at(4 - origin_x, 4 - origin_y), color)
+        key = (origin_x + to_x) % 4 * 4 + (origin_y + to_y) % 4
+        copy = remote(
+            source,
+            source,
+            send_c.at[color, key],
+            recv_c.at[color, key],
+            chip_at(spot_at(to_x, to_y)),
         )
-        for step in range(1, PLANE)
-    ]
-    for copy in sends:
         copy.start()
-    passed = [remote(out_ref.at[group], out_ref.at[group], send_f.at[0], recv_f.at[0], beside)]
-    passed[0].start()
-    for step in range(1, PLANE):
-        sends[step - 1].wait_recv()
-        spot_x = (plane // 4 + 4 - step // 4) % 4
-        spot_y = (plane % 4 + 4 - step % 4) % 4
-        slot = (spot_x * 4 + spot_y) * 2 + core
-        copy = remote(out_ref.at[slot], out_ref.at[slot], send_f.at[step], recv_f.at[step], beside)
+        started.append(copy)
+
+    def landed(origin_x, origin_y, color):
+        key = origin_x * 4 + origin_y
+        part = held(spot_at(4 - origin_x, 4 - origin_y), color)
+        remote(part, part, send_c.at[color, key], recv_c.at[color, key], chip_at(plane)).wait_recv()
+        give(origin_x, origin_y, color)
+
+    def give(origin_x, origin_y, color):
+        key = origin_x * 4 + origin_y
+        part = held(spot_at(4 - origin_x, 4 - origin_y), color)
+        copy = remote(part, part, send_f.at[color, key], recv_f.at[color, key], beside)
         copy.start()
-        passed.append(copy)
-    for copy in sends:
+        passed[color, key] = copy
+
+    passed = {}
+    for turn in (2, 1, 3):
+        forward(0, 0, 0, 0, turn)
+        forward(0, 0, 1, 1, turn)
+    for turn in (2, 1, 3):
+        forward(0, 0, 0, 1, turn)
+        forward(0, 0, 1, 0, turn)
+    for color in range(2):
+        give(0, 0, color)
+
+    lanes = lax.broadcasted_iota(jnp.int32, (L, LANES), 1)
+    pair = 2 * LAGS * L
+
+    def lay(at):
+        both = jnp.concatenate([blocks[2 * at], blocks[2 * at + 1]], axis=1)
+        line[:, pl.ds(pl.multiple_of(M * L + at * pair, LANES), pair)] = both
+        turned = jnp.transpose(both)
+        parts = [turned[L * lag : L * lag + L, :] for lag in range(2 * LAGS - 1, -1, -1)]
+        filler = jnp.zeros((L, L), jnp.float32)
+        tail = jnp.zeros((L, LANES - L), jnp.float32)
+        wide = jnp.concatenate([filler] + parts + [tail], axis=1)
+        start = (PLANE - 1 - at) * pair
+        front = pl.ds(pl.multiple_of(start, LANES), LANES)
+        inner = pl.ds(pl.multiple_of(start + LANES, LANES), pair - LANES)
+        back = pl.ds(pl.multiple_of(start + pair, LANES), LANES)
+        line[:, front] = jnp.where(lanes < L, line[:, front], wide[:, :LANES])
+        line[:, inner] = wide[:, LANES:pair]
+
+        @pl.when(at > 0)
+        def _():
+            line[:, back] = jnp.where(lanes < L, wide[:, pair:], line[:, back])
+
+    def settle(origin_x, origin_y):
+        key = origin_x * 4 + origin_y
+        for color in range(2):
+            passed[color, key].wait()
+        lay(spot_at(4 - origin_x, 4 - origin_y))
+
+    first_wave = (1, 3, 2)
+    for turn in first_wave:
+        landed(turn, 0, 0)
+        for to_turn in (2, 1, 3):
+            forward(turn, 0, 0, 1, to_turn)
+        landed(0, turn, 1)
+        for to_turn in (2, 1, 3):
+            forward(0, turn, 1, 0, to_turn)
+    settle(0, 0)
+    for turn in first_wave:
+        landed(0, turn, 0)
+        landed(turn, 0, 1)
+        settle(0, turn)
+        settle(turn, 0)
+    for turn_x in first_wave:
+        for turn_y in first_wave:
+            landed(turn_x, turn_y, 0)
+            landed(turn_x, turn_y, 1)
+            settle(turn_x, turn_y)
+    for copy in started:
         copy.wait_send()
-    for copy in passed:
-        copy.wait()
 
 
 def lag_blocks(series):
@@ -186,10 +289,11 @@
     dma = pltpu.SemaphoreType.DMA
     return pl.pallas_call(
         lag_kernel,
-        out_shape=jax.ShapeDtypeStruct((2 * PLANE, L, LAGS * L), jnp.float32),
+        out_shape=jax.ShapeDtypeStruct((L, 2 * M * L + 2 * LANES), jnp.float32),
         in_specs=[vmem],
         out_specs=vmem,
         scratch_shapes=[
+            pltpu.VMEM((2 * PLANE, L, LAGS * L), jnp.float32),
             pltpu.VMEM((L, SPAN + 2 * DAYS), jnp.float32),
             pltpu.VMEM((L, SPAN + LANES), jnp.float32),
             pltpu.VMEM((3 * L, SPAN), jnp.bfloat16),
@@ -202,8 +306,10 @@
             dma((PLANE,)),
             dma((PLANE,)),
             dma((PLANE,)),
-            dma((PLANE,)),
-            dma((PLANE,)),
+            dma((2, PLANE)),
+            dma((2, PLANE)),
+            dma((2, PLANE)),
+            dma((2, PLANE)),
             dma((2,)),
             dma((2,)),
         ],
@@ -213,42 +319,29 @@
     )(series)
 
 
-def assemble_kernel(blocks_ref, cov_ref, hi_ref, mid_ref, low_ref, line):
+def assemble_kernel(line, cov_ref, hi_ref, mid_ref, low_ref):
     tm = lax.axis_index("tm")
     panel = lax.axis_index("panel")
     low_z = tm // PLANE
     plane = tm % PLANE
-    step = pl.program_id(0)
-    pair = 2 * LAGS * L
-
-    @pl.when(step == 0)
-    def _():
-        def lay(at, carry):
-            both = jnp.concatenate([blocks_ref[2 * at], blocks_ref[2 * at + 1]], axis=1)
-            line[:, pl.ds(pl.multiple_of(M * L + at * pair, LANES), pair)] = both
-            after = blocks_ref[jnp.minimum(2 * at + 2, 2 * PLANE - 1)][:, :LANES]
-            turned = jnp.transpose(jnp.concatenate([both, after], axis=1))
-            reversed_blocks = [
-                turned[L * lag : L * lag + L, :] for lag in range(2 * LAGS, 0, -1)
-            ]
-            line[:, pl.ds(pl.multiple_of((PLANE - 1 - at) * pair, LANES), pair)] = jnp.concatenate(
-                reversed_blocks, axis=1
-            )
-            return carry
-
-        lax.fori_loop(0, PLANE, lay, 0)
-
+    h = pl.program_id(0)
     own_lag = 3 * (tm * 4 + panel)
-    for offset in range(3):
-        start = L * (M - own_lag - offset) + step * COLS
-        cov_ref[L * offset : L * offset + L, :] = rolled_window(line, start, COLS)
-    h = step // 4
-    spot = step % 4
-    base = L * (372 + (low_z - h) * 192 - 12 * plane + 3 * panel + 12 - 3 * spot - 2)
-    window = rolled_window(line, base, 71 * LANES)
-    for offset in range(3):
+    width = COLS // 2
+
+    def fill(at, carry):
+        spot = h * 8 + at
+        out = pl.ds(pl.multiple_of(at * width, LANES), width)
+        for offset in range(3):
+            start = L * (M - own_lag - offset) + spot * width
+            cov_ref[L * offset : L * offset + L, out] = rolled_window(line, start, width)
+        return carry
+
+    lax.fori_loop(0, 8, fill, 0)
+    base = L * (373 + (low_z - h) * 192 - 12 * plane + 3 * panel)
+    window = rolled_window(line, base, 73 * LANES)
+    for offset in range(12):
         pieces = [
-            window[:, L * (2 - offset + 12 * at) : L * (2 - offset + 12 * at) + ROWS]
+            window[:, L * (11 - offset + 12 * at) : L * (11 - offset + 12 * at) + ROWS]
             for at in range(PLANE)
         ]
         hi, mid, low = split3(jnp.concatenate(pieces, axis=1))
@@ -258,18 +351,17 @@
         low_ref[0, at, :] = low
 
 
-def assemble(blocks):
-    shape = jax.ShapeDtypeStruct((LINE, ROWS, COLS), jnp.bfloat16)
-    spec = pl.BlockSpec((1, ROWS, COLS), lambda h: (h, 0, 0))
+def assemble(line):
+    shape = jax.ShapeDtypeStruct((2, 4 * ROWS, COLS), jnp.bfloat16)
+    spec = pl.BlockSpec((1, 4 * ROWS, COLS), lambda h: (h, 0, 0))
     return pl.pallas_call(
         assemble_kernel,
-        grid=(LINE,),
+        grid=(2,),
         out_shape=(jax.ShapeDtypeStruct((ROWS, M * L), jnp.float32), shape, shape, shape),
-        in_specs=[pl.BlockSpec((2 * PLANE, L, LAGS * L), lambda h: (0, 0, 0))],
-        out_specs=(pl.BlockSpec((ROWS, COLS), lambda h: (0, h)), spec, spec, spec),
-        scratch_shapes=[pltpu.VMEM((L, 2 * M * L + 2 * LANES), jnp.float32)],
-        compiler_params=pltpu.CompilerParams(vmem_limit_bytes=60 * 1024 * 1024),
-    )(blocks)
+        in_specs=[pl.BlockSpec(memory_space=pltpu.VMEM)],
+        out_specs=(pl.BlockSpec((ROWS, M * L // 2), lambda h: (0, h)), spec, spec, spec),
+        compiler_params=pltpu.CompilerParams(vmem_limit_bytes=62 * 1024 * 1024),
+    )(line)
 
 
 def exact_dot(left, right, contract):
@@ -648,8 +740,7 @@
 
 def local(series, start_block):
     covariance, hi, mid, low = assemble(lag_blocks(series))
-    shape = (2, 12 * L, COLS)
-    basis, diag, off = lanczos(start_block, hi.reshape(shape), mid.reshape(shape), low.reshape(shape))
+    basis, diag, off = lanczos(start_block, hi, mid, low)
     return covariance, basis, diag, off
 
 

time: 264 us -> 259 us (0.981)
  Pallas kernels: 257 us -> 252 us
    pallas_call x2, Pallas kernels: 82.3 us -> 78.2 us  [the longest x1 62.6 us: lag_blocks(): pl.pallas_call(lag_kernel, out_shape=jax.ShapeDtypeStruct((L, 2 * M * L +...]
where the time goes in v5:
time: 259 us
  Pallas kernels  252 us (97%)
  local copies, waits for them, and re-layouts  6.09 us (2%)
    pallas_call x1, Pallas kernels, lanczos(): pl.pallas_call(lanczos_kernel, out_shape=(jax.ShapeDtypeStruct((ITERS + 1...  174 us
    pallas_call x1, Pallas kernels, lag_blocks(): pl.pallas_call(lag_kernel, out_shape=jax.ShapeDtypeStruct((L, 2 * M * L +...  62.6 us
    pallas_call x1, Pallas kernels, assemble(): pl.pallas_call(assemble_kernel, grid=(2,), out_shape=(jax.ShapeDtypeStruc...  15.6 us
    unnamed x6, local copies, waits for them, and re-layouts  6.09 us

profile of v5, /device:TPU:1, one launch (start us, length us, event | category | flops | bytes accessed | tf_op | source)
XLA Modules:
  0.0 258.9 jit_solution(8689123187507278340)
XLA Ops:
  0.6 62.6 %shard_map.57.line = f32[48,37120]{1,0:T(8,128)} custom-call(f32[48,256]{1,0:T(8,128)} %series_ref.1), custom_call_target="tpu_custom_call" | custom-call | tf_op jit(solution)/shard_map/pallas_call | solution.py:290
  63.3 0.0 copy-start
  63.3 15.6 %shard_map.58 = (f32[144,18432]{1,0:T(8,128)}, bf16[2,576,2304]{2,1,0:T(8,128)(2,1)}, bf16[2,576,2304]{2,1,0:T(8,128)(2,1)}, bf16[2,576,2304]{2,1,0:T(8,128)(2,1)}) custom-call(f32[48,37120]{1,0:T(8,128)} %shard_map.57.line), custom_call_target="tpu_custom_call" | custom-call | tf_op jit(solution)/shard_map/pallas_call | solution.py:357
  78.8 0.0 copy-done
  78.8 0.7 copy.6.start_ref
  79.6 174.0 %shard_map.59 = (f32[7,144,64]{2,1,0:T(8,128)}, f32[6,64,64]{2,1,0:T(8,128)}, f32[7,64,64]{2,1,0:T(8,128)}) custom-call(f32[144,64]{1,0:T(8,128)} %copy.6.start_ref, bf16[2,576,2304]{2,1,0:T(8,128)(2,1)} %get-tuple-element.12.hi_ref, bf16[2,576,2304]{2,1,0:T(8,128)(2,1)} %get-tuple-element.13.mid_ref, bf16[2,576,2304]{2,1,0:T(8,128)(2,1)} %get-tuple-element.14.low_ref), custom_call_target="tpu_custom_call" | custom-call | tf_op jit(solution)/shard_map/pallas_call | solution.py:695
  253.5 2.1 copy.7
  255.6 1.6 copy.10
  257.2 1.6 copy.11
Async XLA Ops:
  63.3 15.6 %copy-start = (f32[144,64]{0,1:T(8,128)S(1)}, f32[144,64]{0,1:T(8,128)}, u32[]{:S(2)}) copy-start(f32[144,64]{0,1:T(8,128)} %param.3) | copy-start | bytes 110596

commit v6 on v5

--- a/solution.py
+++ b/solution.py
@@ -16,7 +16,6 @@
 PLANE = 16
 LINE = 8
 COLS = PLANE * ROWS
-HALF_COLS = COLS // 2
 LANES = 128
 DAYS = 256
 SPAN = PLANE * DAYS
@@ -381,7 +380,7 @@
     small_lanes = lax.broadcasted_iota(jnp.int32, (B, B), 1)
     identity = jnp.where(small_rows == small_lanes, 1.0, 0.0).astype(jnp.float32)
     work = jnp.concatenate([gram, identity], axis=1)
-    width = 4
+    width = 8
     for first in range(0, B, width):
         columns = [
             jnp.broadcast_to(work[:, first + t : first + t + 1], (B, 2 * B)) for t in range(width)
@@ -401,8 +400,6 @@
     return upper, inverse
 
 
-PAIR_FIRST = [(0, y) for y in (2, 1, 3)] + [(1, y) for y in (2, 1, 3, 0)]
-PAIR_LAST = [(2, y) for y in (2, 1, 3, 0)] + [(3, y) for y in (2, 1, 3, 0)]
 FAR_FIRST = [10, 6, 14, 9, 11, 2, 8, 5, 7, 13, 15, 1, 3, 4, 12]
 
 
@@ -428,10 +425,8 @@
     work,
     current,
     applied,
-    packed,
     gathered,
     stacked,
-    accumulated,
     partial,
     landed,
     gram,
@@ -473,13 +468,6 @@
         spot_p = (panel + step % 4) % 4
         return spot_z * 4 + spot_p, (spot_z * PLANE + plane, spot_p)
 
-    pair_at = plane // 8
-    odd_x = (plane // 4) % 2
-
-    def x_at(turn):
-        side = (pair_at + turn // 2) % 2
-        return side * 2 + (odd_x + turn) % 2
-
     barrier = pltpu.get_barrier_semaphore()
     for step in range(1, PLANE):
         pl.semaphore_signal(barrier, inc=1, device_id=plane_peer(step)[1], device_id_type=MESH)
@@ -506,29 +494,43 @@
         before = current[...]
         rows_block = work[...]
 
-        def block_copies(places, first):
-            found = []
-            for at, (turn, y) in enumerate(places):
-                to_x = x_at(turn)
-                to_y = (plane % 4 + y) % 4
-                from_y = (plane % 4 + 4 - y) % 4
-                to_spot = to_x * 4 + to_y
-                copy = remote(
-                    packed,
-                    gathered.at[slot, plane],
-                    send_q.at[first + at],
-                    recv_q.at[slot, first + at],
-                    (low_z * PLANE + to_spot, panel),
-                )
-                found.append((copy, x_at(turn) * 4 + from_y))
-            return found
-
-        near = [] if last else block_copies(PAIR_FIRST, 0)
-        far = [] if last else block_copies(PAIR_LAST, len(PAIR_FIRST))
+        moved = []
+
+        def part_at(spot, color):
+            return gathered.at[slot, spot, pl.ds(40 * color, 40 - 8 * color)]
+
+        def spot_at(turn_x, turn_y):
+            return ((plane // 4 + turn_x) % 4) * 4 + (plane % 4 + turn_y) % 4
+
+        def forward(origin_x, origin_y, color, along, to_turn):
+            to_x, to_y = (to_turn, 0) if along == 0 else (0, to_turn)
+            part = part_at(spot_at(4 - origin_x, 4 - origin_y), color)
+            key = (origin_x + to_x) % 4 * 4 + (origin_y + to_y) % 4
+            copy = remote(
+                part,
+                part,
+                send_q.at[color, key],
+                recv_q.at[slot, color, key],
+                (low_z * PLANE + spot_at(to_x, to_y), panel),
+            )
+            copy.start()
+            moved.append(copy)
+
+        def await_part(origin_x, origin_y, color):
+            key = origin_x * 4 + origin_y
+            part = part_at(spot_at(4 - origin_x, 4 - origin_y), color)
+            remote(
+                part, part, send_q.at[color, key], recv_q.at[slot, color, key], (tm, panel)
+            ).wait_recv()
+
         if not last:
-            packed[...] = pack(rows_block)
-            for copy, _ in near + far:
-                copy.start()
+            gathered[slot, plane] = pack(rows_block)
+            for turn in (2, 1, 3):
+                forward(0, 0, 0, 0, turn)
+                forward(0, 0, 1, 1, turn)
+            for turn in (2, 1, 3):
+                forward(0, 0, 0, 1, turn)
+                forward(0, 0, 1, 0, turn)
 
         both = jnp.concatenate([before, rows_block], axis=1)
         gram[...] = exact_dot(both, both, ((0,), (0,))).reshape(LINE, 16, 2 * B)
@@ -551,8 +553,16 @@
             at = pl.ds(pl.multiple_of(spot * ROWS, ROWS), ROWS)
             stacked[at, :] = jnp.concatenate([hi, mid, low], axis=1)
 
+        wave = (1, 3, 2)
         if not last:
-            lay(plane, packed[...])
+            lay(plane, gathered[slot, plane])
+            for turn in wave:
+                await_part(turn, 0, 0)
+                for to_turn in (2, 1, 3):
+                    forward(turn, 0, 0, 1, to_turn)
+                await_part(0, turn, 1)
+                for to_turn in (2, 1, 3):
+                    forward(0, turn, 1, 0, to_turn)
         for copy in firsts:
             copy.wait()
         reduced = stage1[0]
@@ -585,15 +595,12 @@
             if not last
         ]
 
-        def multiply(h, half):
-            lanes = pl.ds(pl.multiple_of(half * HALF_COLS, HALF_COLS), HALF_COLS)
-            first = jnp.dot(tile_hi[h, :, lanes], stacked[lanes, :], preferred_element_type=jnp.float32)
+        def multiply(h):
+            first = jnp.dot(tile_hi[h], stacked[...], preferred_element_type=jnp.float32)
             second = jnp.dot(
-                tile_mid[h, :, lanes], stacked[lanes, : 2 * B], preferred_element_type=jnp.float32
+                tile_mid[h], stacked[:, : 2 * B], preferred_element_type=jnp.float32
             )
-            third = jnp.dot(
-                tile_low[h, :, lanes], stacked[lanes, :B], preferred_element_type=jnp.float32
-            )
+            third = jnp.dot(tile_low[h], stacked[:, :B], preferred_element_type=jnp.float32)
             low_part = third + second[:, B:] + first[:, 2 * B :]
             return first[:, :B] + (first[:, B : 2 * B] + second[:, :B] + low_part)
 
@@ -608,31 +615,33 @@
                 landed[slot, line] = partial[line]
 
         def finish(h):
-            product = accumulated[h] + multiply(h, other)
+            product = multiply(h)
             for spot in range(4):
                 rows = product[spot * ROWS : (spot + 1) * ROWS]
                 partial[h * 4 + spot] = pack(rows)
             send_sums(h)
 
-        other = 1 - pair_at
+        def place(origin_x, origin_y):
+            spot = spot_at(4 - origin_x, 4 - origin_y)
+            lay(spot, gathered[slot, spot])
+
         if not last:
-            for copy, spot in near:
-                copy.wait()
-                lay(spot, gathered[slot, spot])
+            for turn in wave:
+                await_part(0, turn, 0)
+                await_part(turn, 0, 1)
+                place(0, turn)
+                place(turn, 0)
+            for turn_x in wave:
+                for turn_y in wave:
+                    await_part(turn_x, turn_y, 0)
+                    await_part(turn_x, turn_y, 1)
+                    place(turn_x, turn_y)
 
             @pl.when(step_at == 0)
             def _():
                 for copy in tiles:
                     copy.wait()
 
-            def begin(h, carry):
-                accumulated[h] = multiply(h, pair_at)
-                return carry
-
-            lax.fori_loop(0, 2, begin, 0)
-            for copy, spot in far:
-                copy.wait()
-                lay(spot, gathered[slot, spot])
             finish(0)
 
         for copy in seconds:
@@ -667,6 +676,8 @@
             return
         for copy in sums:
             copy.wait()
+        for copy in moved:
+            copy.wait_send()
         value = landed[slot, 0]
         for spot in range(1, LINE):
             value = value + landed[slot, spot]
@@ -708,10 +719,8 @@
             pltpu.VMEM((ROWS, B), jnp.float32),
             pltpu.VMEM((ROWS, B), jnp.float32),
             pltpu.VMEM((ROWS, B), jnp.float32),
-            pltpu.VMEM((HALF, 2 * B), jnp.float32),
             pltpu.VMEM((2, PLANE, HALF, 2 * B), jnp.float32),
             pltpu.VMEM((COLS, 3 * B), jnp.bfloat16),
-            pltpu.VMEM((2, 4 * ROWS, B), jnp.float32),
             pltpu.VMEM((LINE, HALF, 2 * B), jnp.float32),
             pltpu.VMEM((2, LINE, HALF, 2 * B), jnp.float32),
             pltpu.VMEM((LINE, 16, 2 * B), jnp.float32),
@@ -721,8 +730,8 @@
             pltpu.VMEM((16, 2 * B), jnp.float32),
             pltpu.VMEM((LINE, 16, 2 * B), jnp.float32),
             dma((3,)),
-            dma((PLANE,)),
             dma((2, PLANE)),
+            dma((2, 2, PLANE)),
             dma((LINE,)),
             dma((2, LINE)),
             dma((LINE,)),

time: 259 us -> 234 us (0.903)
  Pallas kernels: 252 us -> 227 us
    pallas_call x1, Pallas kernels: 174 us -> 149 us  [lanczos(): pl.pallas_call(lanczos_kernel, out_shape=(jax.ShapeDtypeStruct((ITERS + 1...]
where the time goes in v6:
time: 234 us
  Pallas kernels  227 us (97%)
  local copies, waits for them, and re-layouts  6.09 us (3%)
    pallas_call x1, Pallas kernels, lanczos(): pl.pallas_call(lanczos_kernel, out_shape=(jax.ShapeDtypeStruct((ITERS + 1...  149 us
    pallas_call x1, Pallas kernels, lag_blocks(): pl.pallas_call(lag_kernel, out_shape=jax.ShapeDtypeStruct((L, 2 * M * L +...  62.6 us
    pallas_call x1, Pallas kernels, assemble(): pl.pallas_call(assemble_kernel, grid=(2,), out_shape=(jax.ShapeDtypeStruc...  15.6 us
    unnamed x6, local copies, waits for them, and re-layouts  6.09 us

profile of v6, /device:TPU:1, one launch (start us, length us, event | category | flops | bytes accessed | tf_op | source)
XLA Modules:
  0.0 234.2 jit_solution(693390272353221441)
XLA Ops:
  0.6 62.6 %shard_map.57.line = f32[48,37120]{1,0:T(8,128)} custom-call(f32[48,256]{1,0:T(8,128)} %series_ref.1), custom_call_target="tpu_custom_call" | custom-call | tf_op jit(solution)/shard_map/pallas_call | solution.py:289
  63.3 0.0 copy-start
  63.3 15.6 %shard_map.58 = (f32[144,18432]{1,0:T(8,128)}, bf16[2,576,2304]{2,1,0:T(8,128)(2,1)}, bf16[2,576,2304]{2,1,0:T(8,128)(2,1)}, bf16[2,576,2304]{2,1,0:T(8,128)(2,1)}) custom-call(f32[48,37120]{1,0:T(8,128)} %shard_map.57.line), custom_call_target="tpu_custom_call" | custom-call | tf_op jit(solution)/shard_map/pallas_call | solution.py:356
  78.8 0.0 copy-done
  78.8 0.7 copy.6.start_ref
  79.6 149.2 %shard_map.59 = (f32[7,144,64]{2,1,0:T(8,128)}, f32[6,64,64]{2,1,0:T(8,128)}, f32[7,64,64]{2,1,0:T(8,128)}) custom-call(f32[144,64]{1,0:T(8,128)} %copy.6.start_ref, bf16[2,576,2304]{2,1,0:T(8,128)(2,1)} %get-tuple-element.12.hi_ref, bf16[2,576,2304]{2,1,0:T(8,128)(2,1)} %get-tuple-element.13.mid_ref, bf16[2,576,2304]{2,1,0:T(8,128)(2,1)} %get-tuple-element.14.low_ref), custom_call_target="tpu_custom_call" | custom-call | tf_op jit(solution)/shard_map/pallas_call | solution.py:706
  228.8 2.1 copy.7
  230.9 1.6 copy.10
  232.5 1.6 copy.11
Async XLA Ops:
  63.3 15.6 %copy-start = (f32[144,64]{0,1:T(8,128)S(1)}, f32[144,64]{0,1:T(8,128)}, u32[]{:S(2)}) copy-start(f32[144,64]{0,1:T(8,128)} %param.3) | copy-start | bytes 110596

commit v7 on v6

--- a/solution.py
+++ b/solution.py
@@ -223,10 +223,10 @@
         passed[color, key] = copy
 
     passed = {}
-    for turn in (2, 1, 3):
+    for turn in (3, 1):
         forward(0, 0, 0, 0, turn)
         forward(0, 0, 1, 1, turn)
-    for turn in (2, 1, 3):
+    for turn in (3, 1):
         forward(0, 0, 0, 1, turn)
         forward(0, 0, 1, 0, turn)
     for color in range(2):
@@ -260,24 +260,40 @@
             passed[color, key].wait()
         lay(spot_at(4 - origin_x, 4 - origin_y))
 
-    first_wave = (1, 3, 2)
+    first_wave = (3, 1, 2)
     for turn in first_wave:
         landed(turn, 0, 0)
-        for to_turn in (2, 1, 3):
+        landed(0, turn, 1)
+        if turn == 3:
+            forward(3, 0, 0, 0, 3)
+            forward(0, 3, 1, 1, 3)
+        for to_turn in (3, 1):
             forward(turn, 0, 0, 1, to_turn)
-        landed(0, turn, 1)
-        for to_turn in (2, 1, 3):
             forward(0, turn, 1, 0, to_turn)
+        if turn == 3:
+            landed(0, 3, 0)
+            forward(0, 3, 0, 1, 3)
+            landed(3, 0, 1)
+            forward(3, 0, 1, 0, 3)
     settle(0, 0)
     for turn in first_wave:
+        landed(turn, 3, 0)
+        forward(turn, 3, 0, 1, 3)
+        landed(3, turn, 1)
+        forward(3, turn, 1, 0, 3)
+    settle(0, 3)
+    settle(3, 0)
+    for turn in (1, 2):
         landed(0, turn, 0)
         landed(turn, 0, 1)
         settle(0, turn)
         settle(turn, 0)
     for turn_x in first_wave:
         for turn_y in first_wave:
-            landed(turn_x, turn_y, 0)
-            landed(turn_x, turn_y, 1)
+            if turn_y != 3:
+                landed(turn_x, turn_y, 0)
+            if turn_x != 3:
+                landed(turn_x, turn_y, 1)
             settle(turn_x, turn_y)
     for copy in started:
         copy.wait_send()
@@ -747,9 +763,25 @@
     )(start, hi, mid, low)
 
 
+def hand_over_kernel(basis_ref, diag_ref, off_ref, basis_out, diag_out, off_out):
+    basis_out[...] = basis_ref[...]
+    diag_out[...] = diag_ref[...]
+    off_out[...] = off_ref[...]
+
+
+def hand_over(*arrays):
+    vmem = pl.BlockSpec(memory_space=pltpu.VMEM)
+    return pl.pallas_call(
+        hand_over_kernel,
+        out_shape=tuple(jax.ShapeDtypeStruct(x.shape, x.dtype) for x in arrays),
+        in_specs=[vmem] * 3,
+        out_specs=(vmem, vmem, vmem),
+    )(*arrays)
+
+
 def local(series, start_block):
     covariance, hi, mid, low = assemble(lag_blocks(series))
-    basis, diag, off = lanczos(start_block, hi, mid, low)
+    basis, diag, off = hand_over(*lanczos(start_block, hi, mid, low))
     return covariance, basis, diag, off
 
 

time: 234 us -> 235 us (level)
  Pallas kernels: 227 us -> 231 us
  local copies, waits for them, and re-layouts: 6.09 us -> 2.83 us
    unnamed x6 -> x4, local copies, waits for them, and re-layouts: 6.09 us -> 2.83 us
where the time goes in v7:
time: 235 us; the launch traced here: 234 us
  Pallas kernels  231 us (98%)
  local copies, waits for them, and re-layouts  2.83 us (1%)
    pallas_call x1, Pallas kernels, lanczos(): pl.pallas_call(lanczos_kernel, out_shape=(jax.ShapeDtypeStruct((ITERS + 1...  150 us
    pallas_call x1, Pallas kernels, lag_blocks(): pl.pallas_call(lag_kernel, out_shape=jax.ShapeDtypeStruct((L, 2 * M * L +...  63.7 us
    pallas_call x1, Pallas kernels, assemble(): pl.pallas_call(assemble_kernel, grid=(2,), out_shape=(jax.ShapeDtypeStruc...  15.6 us

profile of v7, /device:TPU:1, one launch (start us, length us, event | category | flops | bytes accessed | tf_op | source)
XLA Modules:
  0.0 234.5 jit_solution(12843217232618335917)
XLA Ops:
  0.6 63.7 %shard_map.57.line = f32[48,37120]{1,0:T(8,128)} custom-call(f32[48,256]{1,0:T(8,128)} %series_ref.1), custom_call_target="tpu_custom_call" | custom-call | tf_op jit(solution)/shard_map/pallas_call | solution.py:305
  64.3 0.0 copy-start
  64.3 15.6 %shard_map.58 = (f32[144,18432]{1,0:T(8,128)}, bf16[2,576,2304]{2,1,0:T(8,128)(2,1)}, bf16[2,576,2304]{2,1,0:T(8,128)(2,1)}, bf16[2,576,2304]{2,1,0:T(8,128)(2,1)}) custom-call(f32[48,37120]{1,0:T(8,128)} %shard_map.57.line), custom_call_target="tpu_custom_call" | custom-call | tf_op jit(solution)/shard_map/pallas_call | solution.py:372
  79.9 0.0 copy-done
  79.9 0.7 copy.6.start_ref
  80.6 149.6 %shard_map.59 = (f32[7,144,64]{2,1,0:T(8,128)}, f32[6,64,64]{2,1,0:T(8,128)}, f32[7,64,64]{2,1,0:T(8,128)}) custom-call(f32[144,64]{1,0:T(8,128)} %copy.6.start_ref, bf16[2,576,2304]{2,1,0:T(8,128)(2,1)} %get-tuple-element.15.hi_ref, bf16[2,576,2304]{2,1,0:T(8,128)(2,1)} %get-tuple-element.16.mid_ref, bf16[2,576,2304]{2,1,0:T(8,128)(2,1)} %get-tuple-element.17.low_ref), custom_call_target="tpu_custom_call" | custom-call | tf_op jit(solution)/shard_map/pallas_call | solution.py:722
  230.2 2.1 shard_map.60
  232.4 2.1 copy.7
Async XLA Ops:
  64.3 15.6 %copy-start = (f32[144,64]{0,1:T(8,128)S(1)}, f32[144,64]{0,1:T(8,128)}, u32[]{:S(2)}) copy-start(f32[144,64]{0,1:T(8,128)} %param.3) | copy-start | bytes 110596
